TPU v7x, 128 devices: a whole 4x4x4 slice. The times are simulated.
128 devices in a mesh: sx: 16 (over x, z_hi, core), sy: 8 (over z_lo, y).
Axes of the slice: x: 4, y: 4, z: 4 (z_hi: 2, z_lo: 2; z = z_hi * 2 + z_lo), core: 2. Of those that a mesh axis runs over, the one named last changes fastest.
Arguments:
- tokens: bfloat16 [65536, 1024], P(('sx', 'sy')), may hold values from -6 to 6
- norm_gain: float32 [1024], replicated, may hold values from 0.1 to 1.9
- w_qk: bfloat16 [1024, 1024], replicated, may hold values from -1.75 to 1.75
- w_value: bfloat16 [1024, 1024], replicated, may hold values from -0.1875 to 0.1875
- w_out: bfloat16 [1024, 1024], replicated, may hold values from -0.1875 to 0.1875
- send_order: int32 [8, 65536], P(None, ('sx', 'sy')), may hold values from 0 to 511, as said below
- place: int32 [8, 65536], P(None, ('sx', 'sy')), may hold values from 0 to 511, as said below
Outputs:
- attended: bfloat16 [65536, 1024], P(('sx', 'sy'))
Inputs may be any that keep to these rules, and one draw needn't show every extreme that they name: `send_order`: for every head and every device, the device's 512 entries form a permutation of 0 to 511. `place`: for every head and every device, the device's 512 entries form a permutation of 0 to 511.
All inputs are finite; a program needn't handle non-finite values.
Results may differ from a plain program's by a relative error of at most 0.012.
The roundings to bfloat16 on the way count: a program that leaves them out, or rounds other values in their place, can miss the bound.
Values may be sent and summed in bfloat16 or wider, within the bound.
A program may use at most 64 MiB of HBM per device.

v0:
```python
import jax
import jax.numpy as jnp
from jax import lax
from jax.sharding import PartitionSpec as P

HEADS = 8
HEAD_DIM = 128
SPAN = 128


def shifted(array, axis, by):
    peers = lax.axis_size(axis)
    return lax.ppermute(array, axis, [(i, (i + by) % peers) for i in range(peers)])


def route_out(buffer):
    return lax.all_to_all(buffer, ("sx", "sy"), split_axis=1, concat_axis=1, tiled=True)


def route_back(buffer):
    return lax.all_to_all(buffer, ("sx", "sy"), split_axis=1, concat_axis=1, tiled=True)


def attend_spans(current, previous):
    window = jnp.concatenate([previous, current], axis=2)
    query = current[..., :HEAD_DIM]
    keys = window[..., :HEAD_DIM].astype(jnp.float32)
    key_stat = jnp.sum(keys * keys, -1, keepdims=True) + 1e-06
    unit = (keys * lax.rsqrt(key_stat)).astype(jnp.bfloat16)
    scores = jnp.einsum(
        "hcqd,hckd->hcqk", query, unit, preferred_element_type=jnp.float32
    ) * HEAD_DIM ** (-0.5)
    rows = jnp.arange(SPAN)[:, None]
    cols = jnp.arange(2 * SPAN)[None, :]
    scores = jnp.where(cols == rows + SPAN, -100000.0, scores)
    weights = jax.nn.softmax(scores, axis=-1).astype(jnp.bfloat16)
    return jnp.einsum(
        "hcqk,hckd->hcqd", weights, window[..., HEAD_DIM:], preferred_element_type=jnp.float32
    ).astype(jnp.bfloat16)


def per_device(tokens, norm_gain, w_qk, w_value, w_out, send_order, place):
    tok_rows = tokens.shape[0]
    devices = lax.axis_size(("sx", "sy"))
    peer = tok_rows // devices
    floats = tokens.astype(jnp.float32)
    row_stat = jnp.mean(floats * floats, -1, keepdims=True) + 1e-06
    scale = lax.rsqrt(row_stat)
    normed = (floats * scale * norm_gain).astype(jnp.bfloat16)
    shared = jnp.dot(normed, w_qk, preferred_element_type=jnp.float32).astype(jnp.bfloat16)
    values = jnp.dot(normed, w_value, preferred_element_type=jnp.float32).astype(jnp.bfloat16)
    stacked = jnp.concatenate(
        [shared.reshape(tok_rows, HEADS, HEAD_DIM), values.reshape(tok_rows, HEADS, HEAD_DIM)], -1
    )
    columns = jnp.arange(tok_rows, dtype=jnp.int32)[None, None, :]
    send_table = (send_order[:, :, None] == columns).astype(jnp.bfloat16)
    place_table = (place[:, :, None] == columns).astype(jnp.bfloat16)
    outgoing = jnp.einsum(
        "hit,thc->hic", send_table, stacked, preferred_element_type=jnp.float32
    ).astype(jnp.bfloat16)
    arrived = route_out(outgoing.reshape(HEADS, devices, peer, 2 * HEAD_DIM)).reshape(
        HEADS, tok_rows, 2 * HEAD_DIM
    )
    ordered = jnp.einsum(
        "hip,hic->hpc", place_table, arrived, preferred_element_type=jnp.float32
    ).astype(jnp.bfloat16)
    last_span = ordered[:, tok_rows - SPAN :]
    edge = shifted(last_span, ("sx", "sy"), 1)
    spans = ordered.reshape(HEADS, tok_rows // SPAN, SPAN, 2 * HEAD_DIM)
    previous = jnp.concatenate([edge[:, None], spans[:, :-1]], axis=1)
    sorted_out = attend_spans(spans, previous).reshape(HEADS, tok_rows, HEAD_DIM)
    leaving = jnp.einsum(
        "hip,hpc->hic", place_table, sorted_out, preferred_element_type=jnp.float32
    ).astype(jnp.bfloat16)
    returned = route_back(leaving.reshape(HEADS, devices, peer, HEAD_DIM)).reshape(
        HEADS, tok_rows, HEAD_DIM
    )
    merged = jnp.einsum(
        "hit,hic->thc", send_table, returned, preferred_element_type=jnp.float32
    ).astype(jnp.bfloat16)
    merged = merged.reshape(tok_rows, HEADS * HEAD_DIM)
    return jnp.dot(merged, w_out, preferred_element_type=jnp.float32).astype(jnp.bfloat16)


def solution(mesh):
    return jax.shard_map(
        per_device,
        mesh=mesh,
        in_specs=(
            P(("sx", "sy"), None),
            P(),
            P(),
            P(),
            P(),
            P(None, ("sx", "sy")),
            P(None, ("sx", "sy")),
        ),
        out_specs=P(("sx", "sy"), None),
        check_vma=False,
    )
```

profile of v0, /device:TPU:1, one launch (start us, length us, event | category | flops | bytes accessed | tf_op | source)
XLA Modules:
  0.0 122.5 jit_solution(5686544916147594821)
XLA Ops:
  0.0 0.0 copy-start
  0.0 1.7 %fusion.12 = f32[512]{0:T(512)S(1)} fusion(bf16[512,1024]{1,0:T(8,128)(2,1)} %param.7), kind=kLoop, calls=%fused_computation.22 | loop fusion | flops 1572352 | bytes 1050624 | tf_op jit(solution)/shard_map/reduce_sum | solution.py:47
  1.7 0.2 copy-done
  1.9 0.0 copy-start.2
  1.9 0.0 copy-start.3
  1.9 0.0 copy-start.6
  1.9 2.7 %fusion.37 = bf16[64,8,8,128]{3,2,1,0:T(8,128)(2,1)S(1)} fusion(bf16[1024,1024]{1,0:T(8,128)(2,1)S(1)} %copy-done, bf16[512,1024]{1,0:T(8,128)(2,1)} %param.7, f32[1024]{0:T(1024)} %param.8, f32[512]{0:T(512)S(1)} %add_rsqrt_fusion.1), kind=kOutput, calls=%fused_computation.45 | convolution fusion | flops 1076363264 | bytes 4200448 | tf_op jit(solution)/shard_map/dot_general | solution.py:51
  4.6 0.0 copy-done.2
  4.6 0.0 copy-done.3
  4.6 0.0 copy-done.6
  4.6 1.3 %fusion.36 = bf16[64,8,8,128]{3,2,1,0:T(8,128)(2,1)S(1)} fusion(bf16[1024,1024]{1,0:T(8,128)(2,1)S(1)} %copy-done.3, bf16[512,1024]{1,0:T(8,128)(2,1)S(1)} %copy-done.2, f32[1024]{0:T(1024)S(1)} %copy-done.6, f32[512]{0:T(512)S(1)} %add_rsqrt_fusion.1), kind=kOutput, calls=%fused_computation.44 | convolution fusion | flops 1076363264 | bytes 4200448 | tf_op jit(solution)/shard_map/dot_general | solution.py:50
  5.9 0.0 copy-start.5
  6.0 0.5 copy_bitcast_fusion
  6.5 0.2 copy-done.5
  6.7 2.8 %fusion.27 = bf16[8,512,256]{2,1,0:T(8,128)(2,1)} fusion(bf16[512,8,128]{2,0,1:T(8,128)(2,1)S(1)} %get-tuple-element.7, bf16[512,8,128]{2,0,1:T(8,128)(2,1)S(1)} %get-tuple-element.8, s32[8,512]{1,0:T(8,128)S(1)} %copy-done.5), kind=kOutput, calls=%fused_computation.36 | convolution fusion | flops 1081081856 | bytes 4210688 | tf_op jit(solution)/shard_map/hit,thc->hic/dot_general | solution.py:58
  9.4 4.0 %reshape.53 = bf16[8,128,4,256]{3,2,1,0:T(4,128)(2,1)} reshape(bf16[8,512,256]{2,1,0:T(8,128)(2,1)} %fusion.27) | data formatting | bytes 4194304 | tf_op jit(solution)/shard_map/reshape | solution.py:61
  13.4 2.8 %copy.21 = bf16[8,128,4,256]{3,2,0,1:T(4,128)(2,1)S(1)} copy(bf16[8,128,4,256]{3,2,1,0:T(4,128)(2,1)} %reshape.53) | data formatting | bytes 4194304 | tf_op jit(solution)/shard_map/reshape | solution.py:61
  16.2 41.4 %all_to_all.10 = bf16[8,128,4,256]{3,2,0,1:T(4,128)(2,1)S(1)} all-to-all(bf16[8,128,4,256]{3,2,0,1:T(4,128)(2,1)S(1)} %copy.21), channel_id=1, replica_groups=mesh['sx'=16,'sy'=8] {'sx','sy'}, dimensions={1} | all-to-all | bytes 4194304 | tf_op jit(solution)/shard_map/all_to_all | solution.py:17
  57.6 2.2 %copy.22 = bf16[8,128,4,256]{3,2,1,0:T(4,128)(2,1)} copy(bf16[8,128,4,256]{3,2,0,1:T(4,128)(2,1)S(1)} %all_to_all.10) | data formatting | bytes 4194304 | tf_op jit(solution)/shard_map/all_to_all | solution.py:17
  59.8 0.0 copy-start.4
  59.8 4.0 %reshape.54 = bf16[8,512,256]{2,1,0:T(8,128)(2,1)} reshape(bf16[8,128,4,256]{3,2,1,0:T(4,128)(2,1)} %copy.22) | data formatting | bytes 4194304 | tf_op jit(solution)/shard_map/reshape | solution.py:61
  63.8 0.0 copy-done.4
  63.8 4.4 %fusion.26 = bf16[8,512,256]{2,1,0:T(8,128)(2,1)S(1)} fusion(bf16[8,512,256]{2,1,0:T(8,128)(2,1)} %reshape.54, s32[8,512]{1,0:T(8,128)S(1)} %copy-done.4), kind=kOutput, calls=%fused_computation.35 | convolution fusion | flops 1076887552 | bytes 4210688 | tf_op jit(solution)/shard_map/hip,hic->hpc/dot_general | solution.py:64
  68.2 0.7 collective-permute-start
  68.9 0.1 iota_compare_fusion.14
  69.0 0.1 slice.22
  69.1 14.5 %collective-permute-done = bf16[8,128,256]{2,1,0:T(8,128)(2,1)S(1)} collective-permute-done((bf16[8,128,256]{2,1,0:T(8,128)(2,1)S(1)}, bf16[8,128,256]{2,1,0:T(8,128)(2,1)S(1)}, u32[]{:S(2)}, u32[]{:S(2)}) %collective-permute-start) | collective-permute-done | bytes 524320 | tf_op jit(solution)/shard_map/ppermute | solution.py:13
  83.6 0.5 pad_maximum_fusion
  84.2 1.2 fusion.5
  85.4 3.1 %fusion.15 = f32[8,4,128,256]{3,2,1,0:T(8,128)S(1)} fusion(f32[8,4,256]{2,1,0:T(4,128)S(1)} %add_rsqrt_fusion, bf16[8,4,256,256]{3,2,1,0:T(8,128)(2,1)S(1)} %pad_maximum_fusion, bf16[8,4,128,256]{3,2,1,0:T(8,128)(2,1)S(1)} %bitcast.26), kind=kOutput, calls=%fused_computation.25 | convolution fusion | flops 271581184 | bytes 7372800 | tf_op jit(solution)/shard_map/hcqd,hckd->hcqk/dot_general | solution.py:30
  88.5 2.0 %fusion.45 = (f32[8,4,128]{2,1,0:T(4,128)S(1)}, f32[8,4,128,256]{3,2,1,0:T(8,128)S(1)}) fusion(f32[8,4,128,256]{3,2,1,0:T(8,128)S(1)} %fusion.15, pred[128,256]{1,0:T(8,128)(4,1)S(1)} %iota_compare_fusion.14), kind=kOutput, calls=%fused_computation.57 | output fusion | flops 6291711 | bytes 8437760 | tf_op jit(solution)/shard_map/sub | solution.py:36
  90.5 1.0 fusion.33
  91.5 1.8 %fusion.31 = bf16[8,512,128]{2,1,0:T(8,128)(2,1)S(1)} fusion(bf16[8,512,128]{2,1,0:T(8,128)(2,1)S(1)} %bitcast.31, s32[8,512]{1,0:T(8,128)S(1)} %copy-done.4), kind=kOutput, calls=%fused_computation.38 | convolution fusion | flops 539492352 | bytes 2113536 | tf_op jit(solution)/shard_map/hip,hpc->hic/dot_general | solution.py:72
  93.3 1.2 copy.25
  94.5 23.5 %all_to_all.11 = bf16[8,128,4,128]{3,0,2,1:T(8,128)(2,1)S(1)} all-to-all(bf16[8,128,4,128]{3,0,2,1:T(8,128)(2,1)S(1)} %copy.25), channel_id=1, replica_groups=mesh['sx'=16,'sy'=8] {'sx','sy'}, dimensions={1} | all-to-all | bytes 2097152 | tf_op jit(solution)/shard_map/all_to_all | solution.py:21
  118.0 0.0 copy-start.1
  118.0 2.2 %fusion.32 = bf16[8,128,512]{2,1,0:T(8,128)(2,1)S(1)} fusion(s32[8,512]{1,0:T(8,128)S(1)} %copy-done.5, bf16[8,512,128]{2,0,1:T(8,128)(2,1)S(1)} %bitcast.28), kind=kOutput, calls=%fused_computation.39 | convolution fusion | flops 539492352 | bytes 2113536 | tf_op jit(solution)/shard_map/hit,hic->thc/dot_general | solution.py:78
  120.2 0.0 copy-done.1
  120.2 2.2 %convolution_convert_fusion = bf16[512,1024]{1,0:T(8,128)(2,1)} fusion(bf16[512,1024]{0,1:T(8,128)(2,1)S(1)} %bitcast.29, bf16[1024,1024]{1,0:T(8,128)(2,1)S(1)} %copy-done.1), kind=kOutput, calls=%fused_computation.40 | convolution fusion | flops 1074266112 | bytes 4194304 | tf_op jit(solution)/shard_map/dot_general | solution.py:82
  (4 shorter events, 0.1 us)
Async XLA Ops:
  0.0 1.9 %copy-start = (bf16[1024,1024]{1,0:T(8,128)(2,1)S(1)}, bf16[1024,1024]{1,0:T(8,128)(2,1)}, u32[]{:S(2)}) copy-start(bf16[1024,1024]{1,0:T(8,128)(2,1)} %param.10) | copy-start | bytes 6291460
  1.9 2.7 %copy-start.2 = (bf16[512,1024]{1,0:T(8,128)(2,1)S(1)}, bf16[512,1024]{1,0:T(8,128)(2,1)}, u32[]{:S(2)}) copy-start(bf16[512,1024]{1,0:T(8,128)(2,1)} %param.7) | copy-start | bytes 3145732
  1.9 2.7 %copy-start.3 = (bf16[1024,1024]{1,0:T(8,128)(2,1)S(1)}, bf16[1024,1024]{1,0:T(8,128)(2,1)}, u32[]{:S(2)}) copy-start(bf16[1024,1024]{1,0:T(8,128)(2,1)} %param.9) | copy-start | bytes 6291460
  1.9 2.7 %copy-start.6 = (f32[1024]{0:T(1024)S(1)}, f32[1024]{0:T(1024)}, u32[]{:S(2)}) copy-start(f32[1024]{0:T(1024)} %param.8) | copy-start | bytes 12292
  5.9 0.7 copy-start.5
  59.8 4.0 %copy-start.4 = (s32[8,512]{1,0:T(8,128)S(1)}, s32[8,512]{1,0:T(8,128)}, u32[]{:S(2)}) copy-start(s32[8,512]{1,0:T(8,128)} %param.13) | copy-start | bytes 49156
  68.2 15.4 %collective-permute-start = (bf16[8,128,256]{2,1,0:T(8,128)(2,1)S(1)}, bf16[8,128,256]{2,1,0:T(8,128)(2,1)S(1)}, u32[]{:S(2)}, u32[]{:S(2)}) collective-permute-start(bf16[8,128,256]{2,1,0:T(8,128)(2,1)S(1)} %slice.21), channel_id=1, source_target_pairs={{0,1},{1,2},{2,3},{3,4},{4,5},{5,6},{6,7},{7,8},{8,9},{9,10},{10,1... | collective-permute-start | bytes 1572872 | tf_op jit(solution)/shard_map/ppermute | solution.py:13
  118.0 2.2 %copy-start.1 = (bf16[1024,1024]{1,0:T(8,128)(2,1)S(1)}, bf16[1024,1024]{1,0:T(8,128)(2,1)}, u32[]{:S(2)}) copy-start(bf16[1024,1024]{1,0:T(8,128)(2,1)} %param.11) | copy-start | bytes 6291460
where the time goes:
time: 123 us; the launch traced here: 122 us
  blocking collectives  65 us (53%)
  matrix products  21.5 us (17%)
  local copies, waits for them, and re-layouts  15.3 us (12%)
  waiting for transfers between devices  14.5 us (12%)
  other arithmetic  5.44 us (4%)
    all_to_all x1, blocking collectives, route_out(): lax.all_to_all(buffer, ('sx', 'sy'), split_axis=1, concat_axis=1, tiled=T...  41.4 us
    all_to_all x1, blocking collectives, route_back(): lax.all_to_all(buffer, ('sx', 'sy'), split_axis=1, concat_axis=1, tiled=T...  23.5 us
    ppermute x1, waiting for transfers between devices, shifted(): lax.ppermute(array, axis, [(i, (i + by) % peers) for i in range(peers)])  14.5 us
    reshape x2, local copies, waits for them, and re-layouts, per_device(): outgoing.reshape(HEADS, devices, peer, 2 * HEAD_DIM)  6.74 us
    dot_general x1, matrix products, per_device(): jnp.einsum('hip,hic->hpc', place_table, arrived, preferred_element_type=j...  4.37 us
    reshape x1, local copies, waits for them, and re-layouts, per_device(): route_out(outgoing.reshape(HEADS, devices, peer, 2 * HEAD_DIM))  3.99 us
    dot_general x1, matrix products, attend_spans(): jnp.einsum('hcqd,hckd->hcqk', query, unit, preferred_element_type=jnp.flo...  3.13 us
    dot_general x1, matrix products, per_device(): jnp.einsum('hit,thc->hic', send_table, stacked, preferred_element_type=jn...  2.77 us
  transfers between devices with their start and end apart: 1, of which 1 were waited for; matrix products, arithmetic and copies ran while one was open for 0% of the time, Pallas kernels for 0%

commit v1 on v0

v1 whole, which is shorter than its diff:
```python
import jax
import jax.numpy as jnp
from jax import lax
from jax.experimental import pallas as pl
from jax.experimental.pallas import tpu as pltpu
from jax.sharding import PartitionSpec as P

MESH = pl.DeviceIdType.MESH
F32, BF16, I32 = jnp.float32, jnp.bfloat16, jnp.int32
D, HEADS, HD, SPAN, TOK = 1024, 8, 128, 128, 512
NSX, NSY = 16, 8
NDEV = NSX * NSY
NPOS = 8 * TOK
SCALE = HD ** (-0.5)


def place_of(dxc, dyz):
    sx, sy = lax.axis_index("sx"), lax.axis_index("sy")
    x = lax.rem(sx // 4 + lax.rem(dxc, 4), 4)
    core = lax.rem(lax.rem(sx, 2) + dxc // 4, 2)
    y = lax.rem(lax.rem(sy, 4) + lax.rem(dyz, 4), 4)
    z = lax.rem(lax.rem(sx // 2, 2) * 2 + sy // 4 + dyz // 4, 4)
    return x * 4 + (z // 2) * 2 + core, lax.rem(z, 2) * 4 + y


def signal(sem, target):
    pl.semaphore_signal(sem, inc=1, device_id=target, device_id_type=MESH)


def swapped(rows):
    lane = lax.broadcasted_iota(I32, rows.shape, 1)
    width = rows.shape[1]
    return jnp.where((lane // 4) % 2 == 0, pltpu.roll(rows, width - 4, 1), pltpu.roll(rows, 4, 1))


def spread(columns, out_ref):
    for j in range(8):
        out_ref[j] = jnp.broadcast_to(columns[:, j : j + 1], (TOK, 128))


def hot_rows(column):
    lane = lax.broadcasted_iota(I32, (TOK, 128), 1)
    return jnp.concatenate(
        [jnp.where(column == lane + 128 * c, 1.0, 0.0).astype(BF16) for c in range(TOK // 128)], axis=1
    )


def hot_columns(row):
    token = lax.broadcasted_iota(I32, (TOK, TOK), 0)
    return jnp.where(token == row, 1.0, 0.0).astype(BF16)


def dot(a, b):
    return jnp.dot(a, b, preferred_element_type=F32)


def halves(first, second):
    low = lax.broadcasted_iota(I32, first.shape, 1) < 4
    return jnp.where(low, first, second)


def kernel(
    tokens_hbm, gain_ref, wqk_hbm, wv_hbm, wo_hbm, send_ref, place_ref, out_ref,
    tokens, wqk, wv, wo, normed, outgoing, arrived, leaving, returned, placein, placerow,
    sendcol, placecol, sendrow, mergehot, orderhot, leavehot, ordered, unit, sorted_out, merged,
    load_sem, met_sem, place_s, place_r, out_s, out_r, halo_s, halo_r, back_s, back_r,
):
    sx, sy = lax.axis_index("sx"), lax.axis_index("sy")
    me = sx * NSY + sy

    barrier = pltpu.get_barrier_semaphore()
    for dxc in range(1, 8):
        signal(barrier, place_of(dxc, 0))
    for dyz in range(1, 16):
        signal(barrier, place_of(0, dyz))

    loads = [
        pltpu.make_async_copy(src, dst, load_sem.at[n])
        for n, (src, dst) in enumerate([(tokens_hbm, tokens), (wqk_hbm, wqk), (wv_hbm, wv), (wo_hbm, wo)])
    ]
    for load in loads:
        load.start()

    send = send_ref[...]
    send = jnp.where(lax.rem(sy, 2) == 1, swapped(send), send)
    sendrow[...] = send
    spread(send.T, sendcol)

    loads[0].wait()

    def norm(i, _):
        at = pl.ds(pl.multiple_of(i * 64, 64), 64)
        rows = tokens[at, :].astype(F32)
        stat = jnp.mean(rows * rows, -1, keepdims=True) + 1e-06
        normed[at, :] = (rows * lax.rsqrt(stat) * gain_ref[...]).astype(BF16)
        return 0

    lax.fori_loop(0, TOK // 64, norm, 0)
    loads[1].wait()
    loads[2].wait()

    def project(h, _):
        at = pl.ds(pl.multiple_of(h * HD, HD), HD)
        weight = jnp.concatenate([wqk[:, at], wv[:, at]], axis=1)
        both = dot(normed[...], weight).astype(BF16)
        outgoing[h] = dot(hot_rows(sendcol[h]), both).astype(BF16)
        return 0

    lax.fori_loop(0, HEADS, project, 0)

    pl.semaphore_wait(barrier, 7 + 15)
    for dxc in range(1, 8):
        signal(met_sem, place_of(dxc, 0))

    def send_place(k, _):
        pltpu.make_async_remote_copy(
            place_ref, placein.at[sy], place_s, place_r, device_id=(sx, lax.rem(sy + k, NSY)), device_id_type=MESH
        ).start()
        return 0

    lax.fori_loop(1, NSY, send_place, 0)
    placein[sy] = place_ref[...]

    def send_rows(tx, ty):
        pltpu.make_async_remote_copy(
            outgoing.at[ty, pl.ds(pl.multiple_of(tx * 32, 32), 32)],
            arrived.at[me],
            out_s,
            out_r,
            device_id=(tx, ty),
            device_id_type=MESH,
        ).start()

    def send_near(i, _):
        send_rows(*place_of(i, 0))
        return 0

    def send_plane(i, _):
        send_rows(*place_of(0, i))
        return 0

    def send_far(i, _):
        send_rows(*place_of(1 + lax.rem(i, 7), 1 + lax.rem(i, 15)))
        return 0

    lax.fori_loop(1, 8, send_near, 0)
    lax.fori_loop(1, 16, send_plane, 0)
    pl.semaphore_wait(met_sem, 7)
    lax.fori_loop(0, 105, send_far, 0)
    arrived[me] = outgoing[sy, pl.ds(pl.multiple_of(sx * 32, 32), 32), :]

    def table(h, _):
        mergehot[h] = hot_columns(sendrow[pl.ds(h, 1), :])
        return 0

    lax.fori_loop(0, HEADS, table, 0)
    whole_place = pltpu.make_async_remote_copy(
        placein.at[pl.ds(0, NSY - 1)], placein.at[pl.ds(0, NSY - 1)], place_s, place_r, device_id=(sx, sy),
        device_id_type=MESH,
    )
    whole_place.wait_send()
    whole_place.wait_recv()
    for j in range(8):
        placerow[j : j + 1, :] = placein[j, pl.ds(sy, 1), :]
    block = lax.broadcasted_iota(I32, (8, TOK), 0)
    placerow[...] = jnp.where(block % 2 == 1, swapped(placerow[...]), placerow[...])
    spread(placerow[...].T, placecol)

    def place_table(j, _):
        orderhot[j] = hot_columns(placerow[pl.ds(j, 1), :])
        leavehot[j] = hot_rows(placecol[j])
        return 0

    lax.fori_loop(0, 8, place_table, 0)

    whole_out = pltpu.make_async_remote_copy(
        arrived.at[pl.ds(0, NDEV - 1)], arrived.at[pl.ds(0, NDEV - 1)], out_s, out_r, device_id=(sx, sy),
        device_id_type=MESH,
    )
    whole_out.wait_send()
    whole_out.wait_recv()

    def order(n, _):
        half = 1 - n
        rows = arrived[:, pl.ds(pl.multiple_of(half * 16, 16), 16), :].astype(F32)
        for sub in (1, 0):
            group = rows[:, sub * 8 : sub * 8 + 8, :].reshape(NDEV // 2, 2, 8, 2 * HD)
            even, odd = group[:, 0], group[:, 1]
            for b, pair in ((1, (odd, even)), (0, (even, odd))):
                j = half * 4 + sub * 2 + b
                mixed = halves(*pair).reshape(TOK, 2 * HD).astype(BF16)
                at = pl.ds(pl.multiple_of(SPAN + j * TOK, SPAN), TOK)
                ordered[at, :] = dot(orderhot[j], mixed).astype(BF16)
        return 0

    lax.fori_loop(0, 2, order, 0)
    halo = pltpu.make_async_remote_copy(
        ordered.at[pl.ds(NPOS, SPAN)], ordered.at[pl.ds(0, SPAN)], halo_s, halo_r,
        device_id=(lax.rem(sx + 1, NSX), sy), device_id_type=MESH,
    )
    halo.start()

    def units(i, _):
        at = pl.ds(pl.multiple_of(i * SPAN, SPAN), SPAN)
        keys = ordered[at, :HD].astype(F32)
        stat = jnp.sum(keys * keys, -1, keepdims=True) + 1e-06
        unit[at, :] = (keys * lax.rsqrt(stat)).astype(BF16)
        return 0

    def attend(c, _):
        at = pl.ds(pl.multiple_of(c * SPAN, SPAN), 2 * SPAN)
        query = ordered[pl.ds(pl.multiple_of(c * SPAN + SPAN, SPAN), SPAN), :HD]
        scores = lax.dot_general(query, unit[at, :], (((1,), (1,)), ((), ())), preferred_element_type=F32) * SCALE
        rows = lax.broadcasted_iota(I32, (SPAN, 2 * SPAN), 0)
        cols = lax.broadcasted_iota(I32, (SPAN, 2 * SPAN), 1)
        scores = jnp.where(cols == rows + SPAN, -100000.0, scores)
        peak = jnp.max(scores, -1, keepdims=True)
        grown = jnp.exp(scores - peak)
        weights = (grown / jnp.sum(grown, -1, keepdims=True)).astype(BF16)
        sorted_out[pl.ds(pl.multiple_of(c * SPAN, SPAN), SPAN), :] = dot(weights, ordered[at, HD:]).astype(BF16)
        return 0

    lax.fori_loop(1, 33, units, 0)
    lax.fori_loop(1, 32, attend, 0)
    halo.wait_send()
    halo.wait_recv()
    units(0, 0)
    attend(0, 0)

    def leave(half, _):
        tiles = []
        for sub in range(2):
            parts = []
            for b in range(2):
                j = half * 4 + sub * 2 + b
                rows = sorted_out[pl.ds(pl.multiple_of(j * TOK, TOK), TOK), :]
                parts.append(dot(leavehot[j], rows).reshape(NDEV // 2, 8, HD))
            pair = jnp.stack([halves(parts[0], parts[1]), halves(parts[1], parts[0])], axis=1)
            tiles.append(pair.reshape(NDEV, 8, HD))
        leaving[:, pl.ds(pl.multiple_of(half * 16, 16), 16), :] = jnp.concatenate(tiles, axis=1).astype(BF16)
        return 0

    lax.fori_loop(0, 2, leave, 0)

    def send_back(tx, ty):
        pltpu.make_async_remote_copy(
            leaving.at[tx * NSY + ty],
            returned.at[sy, pl.ds(pl.multiple_of(sx * 32, 32), 32)],
            back_s,
            back_r,
            device_id=(tx, ty),
            device_id_type=MESH,
        ).start()

    def back_far(i, _):
        send_back(*place_of(1 + lax.rem(i, 7), 1 + lax.rem(i, 15)))
        return 0

    def back_near(i, _):
        send_back(*place_of(i, 0))
        return 0

    def back_plane(i, _):
        send_back(*place_of(0, i))
        return 0

    lax.fori_loop(0, 105, back_far, 0)
    lax.fori_loop(1, 16, back_plane, 0)
    lax.fori_loop(1, 8, back_near, 0)
    returned[sy, pl.ds(pl.multiple_of(sx * 32, 32), 32), :] = leaving[me]
    loads[3].wait()
    whole_back = pltpu.make_async_remote_copy(
        leaving.at[pl.ds(0, NDEV - 1)], leaving.at[pl.ds(0, NDEV - 1)], back_s, back_r, device_id=(sx, sy),
        device_id_type=MESH,
    )
    whole_back.wait_send()
    whole_back.wait_recv()

    def merge(h, _):
        merged[:, pl.ds(pl.multiple_of(h * HD, HD), HD)] = dot(mergehot[h], returned[h]).astype(BF16)
        return 0

    lax.fori_loop(0, HEADS, merge, 0)

    def project_out(n, _):
        at = pl.ds(pl.multiple_of(n * 256, 256), 256)
        out_ref[:, at] = dot(merged[...], wo[:, at]).astype(BF16)
        return 0

    lax.fori_loop(0, D // 256, project_out, 0)


def per_device(tokens, norm_gain, w_qk, w_value, w_out, send_order, place):
    vmem = pl.BlockSpec(memory_space=pltpu.VMEM)
    hbm = pl.BlockSpec(memory_space=pl.ANY)
    dma = pltpu.SemaphoreType.DMA
    return pl.pallas_call(
        kernel,
        out_shape=jax.ShapeDtypeStruct((TOK, D), BF16),
        in_specs=[hbm, vmem, hbm, hbm, hbm, vmem, vmem],
        out_specs=vmem,
        scratch_shapes=[
            pltpu.VMEM((TOK, D), BF16),
            pltpu.VMEM((D, D), BF16),
            pltpu.VMEM((D, D), BF16),
            pltpu.VMEM((D, D), BF16),
            pltpu.VMEM((TOK, D), BF16),
            pltpu.VMEM((HEADS, TOK, 2 * HD), BF16),
            pltpu.VMEM((NDEV, 32, 2 * HD), BF16),
            pltpu.VMEM((NDEV, 32, HD), BF16),
            pltpu.VMEM((HEADS, TOK, HD), BF16),
            pltpu.VMEM((NSY, HEADS, TOK), I32),
            pltpu.VMEM((8, TOK), I32),
            pltpu.VMEM((8, TOK, 128), I32),
            pltpu.VMEM((8, TOK, 128), I32),
            pltpu.VMEM((8, TOK), I32),
            pltpu.VMEM((HEADS, TOK, TOK), BF16),
            pltpu.VMEM((8, TOK, TOK), BF16),
            pltpu.VMEM((8, TOK, TOK), BF16),
            pltpu.VMEM((NPOS + SPAN, 2 * HD), BF16),
            pltpu.VMEM((NPOS + SPAN, HD), BF16),
            pltpu.VMEM((NPOS, HD), BF16),
            pltpu.VMEM((TOK, D), BF16),
            dma((4,)),
            pltpu.SemaphoreType.REGULAR,
            dma, dma, dma, dma, dma, dma, dma, dma,
        ],
        compiler_params=pltpu.CompilerParams(
            collective_id=0, has_side_effects=True, vmem_limit_bytes=60 * 2**20
        ),
    )(tokens, norm_gain.reshape(1, D), w_qk, w_value, w_out, send_order, place)


def solution(mesh):
    return jax.shard_map(
        per_device,
        mesh=mesh,
        in_specs=(P(("sx", "sy"), None), P(), P(), P(), P(), P(None, ("sx", "sy")), P(None, ("sx", "sy"))),
        out_specs=P(("sx", "sy"), None),
        check_vma=False,
    )
```

time: 123 us -> 87.6 us (0.71)
  Pallas kernels: 0 us -> 85.1 us
  blocking collectives: 65 us -> 0 us
  matrix products: 21.5 us -> 0 us
  waiting for transfers between devices: 14.5 us -> 0 us
  local copies, waits for them, and re-layouts: 15.3 us -> 2.26 us
  other arithmetic: 5.44 us -> 0 us
    pallas_call x0 -> x1, Pallas kernels: none -> 85.1 us  [per_device(): pl.pallas_call(kernel, out_shape=jax.ShapeDtypeStruct((TOK, D), BF16), in...]
    all_to_all x2 -> x0, blocking collectives: 65 us -> none  [the longest x1 41.4 us: route_out(): lax.all_to_all(buffer, ('sx', 'sy'), split_axis=1, concat_axis=1, tiled=T...]
    dot_general x9 -> x0, matrix products: 21.5 us -> none  [the longest x1 4.37 us: per_device(): jnp.einsum('hip,hic->hpc', place_table, arrived, preferred_element_type=j...]
    ppermute x1 -> x0, waiting for transfers between devices: 14.5 us -> none  [shifted(): lax.ppermute(array, axis, [(i, (i + by) % peers) for i in range(peers)])]
    reshape x5 -> x0, local copies, waits for them, and re-layouts: 12.4 us -> none  [the longest x2 6.74 us: per_device(): outgoing.reshape(HEADS, devices, peer, 2 * HEAD_DIM)]
    reduce_sum x2 -> x0, other arithmetic: 2.82 us -> none  [the longest x1 1.65 us: per_device(): row_stat = jnp.mean(floats * floats, -1, keepdims=True) + 1e-06]
    all_to_all x1 -> x0, local copies, waits for them, and re-layouts: 2.16 us -> none  [route_out(): lax.all_to_all(buffer, ('sx', 'sy'), split_axis=1, concat_axis=1, tiled=T...]
    sub x1 -> x0, other arithmetic: 2 us -> none  [attend_spans(): weights = jax.nn.softmax(scores, axis=-1).astype(jnp.bfloat16)]
  transfers between devices with their start and end apart: 1 -> 0, of which waited for: 1 -> 0; matrix products, arithmetic and copies ran while one was open for 0% -> 0% of each run, Pallas kernels for 0% -> 0%
where the time goes in v1:
time: 87.6 us; the launch traced here: 87.4 us
  Pallas kernels  85.1 us (97%)
  local copies, waits for them, and re-layouts  2.26 us (3%)
    pallas_call x1, Pallas kernels, per_device(): pl.pallas_call(kernel, out_shape=jax.ShapeDtypeStruct((TOK, D), BF16), in...  85.1 us
    unnamed x1, local copies, waits for them, and re-layouts  2.26 us

profile of v1, /device:TPU:1, one launch (start us, length us, event | category | flops | bytes accessed | tf_op | source)
XLA Modules:
  0.0 87.4 jit_solution(604482341412412500)
XLA Ops:
  0.0 85.1 %shard_map.73 = bf16[512,1024]{1,0:T(8,128)(2,1)} custom-call(bf16[512,1024]{1,0:T(8,128)(2,1)} %tokens_hbm.1, f32[1,1024]{1,0:T(1,128)} %bitcast.1, bf16[1024,1024]{1,0:T(8,128)(2,1)} %wqk_hbm.1, bf16[1024,1024]{1,0:T(8,128)(2,1)} %wv_hbm.1, bf16[1024,1024]{1,0:T(8,128)(2,1)} %wo_hbm.1, s32[8,512]{1,0:T(8,128)} %send_ref.1, s32[8,512]{1,0:T(8,128)} %place_ref.1), custom_call_target="tpu_custom_call" | custom-call | tf_op jit(solution)/shard_map/pallas_call | solution.py:297
  85.1 2.3 %copy.9 = bf16[512,1024]{1,0:T(8,128)(2,1)} copy(bf16[512,1024]{1,0:T(8,128)(2,1)} %shard_map.73) | data formatting | bytes 2097152

commit v2 on v0

v2 whole, which is shorter than its diff:
```python
import random

import jax
import jax.numpy as jnp
from jax import lax
from jax.experimental import pallas as pl
from jax.experimental.pallas import tpu as pltpu
from jax.sharding import PartitionSpec as P

MESH = pl.DeviceIdType.MESH
F32, BF16, I32 = jnp.float32, jnp.bfloat16, jnp.int32
D, HEADS, HD, SPAN, TOK = 1024, 8, 128, 128, 512
NSX, NSY = 16, 8
NDEV = NSX * NSY
NPOS = 8 * TOK
GROUP = 4
VMEM_LIMIT = 44 * 2**20
SCALE = HD ** (-0.5)
LOG2E = 1.4426950408889634
scope = jax.named_scope


def offsets():
    every = [
        (dx, hi, core, lo, dy)
        for dx in range(4) for hi in range(2) for core in range(2) for lo in range(2) for dy in range(4)
    ][1:]
    random.Random(1).shuffle(every)
    every.sort(key=lambda o: -(min(o[0], 4 - o[0]) + min(o[4], 4 - o[4]) + (1 if o[3] else 2 * o[1])))
    return [o for o in every if not (o[3] or o[4])], [o for o in every if o[3] or o[4]]


def reach(sx, sy):
    xs = [lax.rem(sx // 4 + d, 4) * 4 for d in range(4)]
    hi, core, lo = lax.rem(sx // 2, 2), lax.rem(sx, 2), sy // 4
    pairs = [[(1 - hi if a else hi) * 2 + (1 - core if b else core) for b in range(2)] for a in range(2)]
    txs = [[[xs[d] + pairs[a][b] for b in range(2)] for a in range(2)] for d in range(4)]
    tys = [[(1 - lo if a else lo) * 4 + lax.rem(lax.rem(sy, 4) + d, 4) for d in range(4)] for a in range(2)]
    return lambda o: (txs[o[0]][o[1]][o[2]], tys[o[3]][o[4]])


def signal(sem, target):
    pl.semaphore_signal(sem, inc=1, device_id=target, device_id_type=MESH)


def swapped(rows):
    lane = lax.broadcasted_iota(I32, rows.shape, 1)
    width = rows.shape[1]
    return jnp.where((lane // 4) % 2 == 0, pltpu.roll(rows, width - 4, 1), pltpu.roll(rows, 4, 1))


def spread(columns, out_ref):
    for j in range(8):
        out_ref[j] = jnp.broadcast_to(columns[:, j : j + 1], (TOK, 128))


def hot_rows(column):
    lane = lax.broadcasted_iota(I32, (TOK, 128), 1)
    return jnp.concatenate(
        [jnp.where(column == lane + 128 * c, 1.0, 0.0).astype(BF16) for c in range(TOK // 128)], axis=1
    )


def hot_columns(row):
    token = lax.broadcasted_iota(I32, (TOK, row.shape[1]), 0)
    return jnp.where(token == row, 1.0, 0.0).astype(BF16)


def dot(a, b):
    return jnp.dot(a, b, preferred_element_type=F32)


def halves(first, second):
    low = lax.broadcasted_iota(I32, first.shape, 1) < 4
    return jnp.where(low, first, second)


def kernel(
    tokens_hbm, gain_hbm, wqk_hbm, wv_hbm, send_hbm, place_hbm, merged,
    tokens, gain, wqk, wv, send_ref, place_ref, normed, outgoing, arrived, leaving, returned, placeout, placein, placerow,
    sendcol, placecol, sendrow, mergehot, orderhot, leavehot, ordered, unit, sorted_out,
    load_sem, met_sem, place_s, place_r, out_s, out_r, halo_s, halo_r, back_s, back_r,
):
    sx, sy = lax.axis_index("sx"), lax.axis_index("sy")
    me = sx * NSY + sy
    at_offset = reach(sx, sy)
    line, rest = offsets()

    with scope("signal"):
        barrier = pltpu.get_barrier_semaphore()
        for k in range(1, NSX):
            signal(barrier, (lax.rem(sx + k, NSX), sy))
        for k in range(1, NSY):
            signal(barrier, (sx, lax.rem(sy + k, NSY)))
        loads = [
            pltpu.make_async_copy(src, dst, load_sem.at[n])
            for n, (src, dst) in enumerate([
                (send_hbm, send_ref), (place_hbm, place_ref), (gain_hbm, gain),
                (tokens_hbm, tokens), (wqk_hbm, wqk), (wv_hbm, wv),
            ])
        ]
        for load in loads:
            load.start()

    with scope("index"):
        loads[0].wait()
        loads[1].wait()
        send = send_ref[...]
        send = jnp.where(lax.rem(sy, 2) == 1, swapped(send), send)
        sendrow[...] = send
        spread(send.T, sendcol)
        for h in range(HEADS):
            placeout[h] = place_ref[h : h + 1, :]

    with scope("norm"):
        loads[2].wait()
        loads[3].wait()

        def norm(i, _):
            at = pl.ds(pl.multiple_of(i * 128, 128), 128)
            rows = tokens[at, :].astype(F32)
            stat = jnp.mean(rows * rows, -1, keepdims=True) + 1e-06
            normed[at, :] = (rows * lax.rsqrt(stat) * gain[...]).astype(BF16)
            return 0

        lax.fori_loop(0, TOK // 128, norm, 0)

    with scope("waitw"):
        loads[4].wait()
        loads[5].wait()

    def project(lo, dy):
        h = at_offset((0, 0, 0, lo, dy))[1]
        at = pl.ds(pl.multiple_of(h * HD, HD), HD)
        weight = jnp.concatenate([wqk[:, at], wv[:, at]], axis=1)
        both = dot(normed[...], weight).astype(BF16)
        rows = dot(hot_rows(sendcol[h]), both)
        outgoing[h] = rows.reshape(NSX, 4, 8, 2 * HD).astype(BF16)

    def send_rows(first, count, sem, target):
        tx, ty = target
        pltpu.make_async_remote_copy(
            outgoing.at[ty, tx, pl.ds(first, count)],
            arrived.at[me, pl.ds(first, count)],
            out_s.at[sem],
            out_r.at[sem],
            device_id=target,
            device_id_type=MESH,
        ).start()

    with scope("project0"):
        project(0, 0)

    with scope("barrier1"):
        pl.semaphore_wait(barrier, NSX - 1 + NSY - 1)
        for k in range(1, NSY):
            signal(met_sem, (sx, lax.rem(sy + k, NSY)))

    with scope("send_near"):
        for o in line:
            send_rows(1, 3, 0, at_offset(o))
        for k in range(1, NSY):
            ty = lax.rem(sy + k, NSY)
            pltpu.make_async_remote_copy(
                placeout.at[ty], placein.at[sy], place_s, place_r, device_id=(sx, ty), device_id_type=MESH
            ).start()

    with scope("project1"):
        for dy in (1, 2, 3):
            project(0, dy)

    with scope("barrier2"):
        pl.semaphore_wait(met_sem, NSY - 1)

    with scope("send_mid"):
        for o in [o for o in rest if not o[3]]:
            send_rows(1, 3, 0, at_offset(o))

    with scope("project2"):
        for dy in range(4):
            project(1, dy)

    with scope("send_far"):
        for o in [o for o in rest if o[3]]:
            send_rows(1, 3, 0, at_offset(o))
        for o in rest + line:
            send_rows(0, 1, 1, at_offset(o))
        arrived[me] = outgoing[sy, sx]

    with scope("tables"):
        def table(h, _):
            mergehot[h] = hot_columns(sendrow[pl.ds(h, 1), :])
            return 0

        lax.fori_loop(0, HEADS, table, 0)
        whole_place = pltpu.make_async_remote_copy(
            placein.at[pl.ds(0, NSY - 1)], placein.at[pl.ds(0, NSY - 1)], place_s, place_r, device_id=(sx, sy),
            device_id_type=MESH,
        )
        whole_place.wait_send()
        whole_place.wait_recv()
        placein[sy] = placeout[sy]
        for j in range(8):
            placerow[j : j + 1, :] = placein[j]
        block = lax.broadcasted_iota(I32, (8, TOK), 0)
        placerow[...] = jnp.where(block % 2 == 1, swapped(placerow[...]), placerow[...])
        spread(placerow[...].T, placecol)

        def place_table(j, _):
            orderhot[j] = hot_columns(placerow[pl.ds(j, 1), :])
            leavehot[j] = hot_rows(placecol[j])
            return 0

        lax.fori_loop(0, 8, place_table, 0)

    def wait_all(ref, send_sem, recv_sem):
        whole = pltpu.make_async_remote_copy(
            ref, ref, send_sem, recv_sem, device_id=(sx, sy), device_id_type=MESH
        )
        whole.wait_send()
        whole.wait_recv()

    def units(keys, at):
        stat = jnp.sum(keys * keys, -1, keepdims=True) + 1e-06
        unit[at, :] = (keys * lax.rsqrt(stat)).astype(BF16)

    def order(q):
        group = arrived[:, q].astype(F32).reshape(NDEV // 2, 2, 8, 2 * HD)
        even, odd = group[:, 0], group[:, 1]
        for b, pair in ((1, (odd, even)), (0, (even, odd))):
            j = 2 * q + b
            mixed = halves(*pair).reshape(TOK, 2 * HD).astype(BF16)
            at = pl.ds(SPAN + j * TOK, TOK)
            rows = dot(orderhot[j], mixed)
            ordered[at, :] = rows.astype(BF16)
            units(rows[:, :HD], at)

    def attend(g, _):
        diagonal = lax.broadcasted_iota(I32, (SPAN, SPAN), 0) == lax.broadcasted_iota(I32, (SPAN, SPAN), 1)
        for u in range(GROUP):
            c = g * GROUP + u
            at = pl.ds(pl.multiple_of(c * SPAN, SPAN), 2 * SPAN)
            query = ordered[pl.ds(pl.multiple_of(c * SPAN + SPAN, SPAN), SPAN), :HD]
            scores = lax.dot_general(query, unit[at, :], (((1,), (1,)), ((), ())), preferred_element_type=F32)
            before, own = scores[:, :SPAN], jnp.where(diagonal, -100000.0 / SCALE, scores[:, SPAN:])
            peak = jnp.max(jnp.maximum(before, own), -1, keepdims=True)
            before, own = jnp.exp2((before - peak) * (SCALE * LOG2E)), jnp.exp2((own - peak) * (SCALE * LOG2E))
            share = 1.0 / jnp.sum(before + own, -1, keepdims=True)
            weights = jnp.concatenate([before * share, own * share], axis=1).astype(BF16)
            sorted_out[pl.ds(pl.multiple_of(c * SPAN, SPAN), SPAN), :] = dot(weights, ordered[at, HD:]).astype(BF16)
        return 0

    def leave(q):
        parts = []
        for b in range(2):
            j = q * 2 + b
            rows = sorted_out[pl.ds(j * TOK, TOK), :]
            parts.append(dot(leavehot[j], rows).reshape(NDEV // 2, 8, HD))
        pair = jnp.stack([halves(parts[0], parts[1]), halves(parts[1], parts[0])], axis=1)
        leaving[:, q] = pair.reshape(NDEV, 8, HD).astype(BF16)

    def send_back(first, target, sem):
        tx, ty = target
        pltpu.make_async_remote_copy(
            leaving.at[tx * NSY + ty, pl.ds(first, 2)],
            returned.at[sy, sx, pl.ds(first, 2)],
            back_s.at[sem],
            back_r.at[sem],
            device_id=target,
            device_id_type=MESH,
        ).start()

    def send_all_back(first, sem):
        for o in rest + line:
            send_back(first, at_offset(o), sem)

    with scope("wait_out0"):
        wait_all(arrived.at[pl.ds(0, NDEV - 1), pl.ds(0, 3)], out_s.at[0], out_r.at[0])

    with scope("order0"):
        order(3)
        halo = pltpu.make_async_remote_copy(
            ordered.at[pl.ds(NPOS, SPAN)], ordered.at[pl.ds(0, SPAN)], halo_s, halo_r,
            device_id=(lax.rem(sx + 1, NSX), sy), device_id_type=MESH,
        )
        halo.start()
        order(2)
        order(1)

    with scope("attend0"):
        lax.fori_loop(12 // GROUP, 32 // GROUP, attend, 0)

    with scope("leave0"):
        leave(3)
        leave(2)

    with scope("back0"):
        send_all_back(2, 0)

    with scope("wait_out1"):
        wait_all(arrived.at[pl.ds(0, NDEV - 1), pl.ds(0, 1)], out_s.at[1], out_r.at[1])

    with scope("order1"):
        order(0)
        halo.wait_send()
        halo.wait_recv()
        units(ordered[pl.ds(0, SPAN), :HD].astype(F32), pl.ds(0, SPAN))

    with scope("attend1"):
        lax.fori_loop(0, 12 // GROUP, attend, 0)

    with scope("leave1"):
        leave(1)
        leave(0)

    with scope("back1"):
        send_all_back(0, 1)
        returned[sy, sx] = leaving[me]

    with scope("wait_back0"):
        wait_all(leaving.at[pl.ds(0, NDEV - 1), pl.ds(0, 2)], back_s.at[0], back_r.at[0])
    with scope("wait_back1"):
        wait_all(leaving.at[pl.ds(0, NDEV - 1), pl.ds(0, 2)], back_s.at[1], back_r.at[1])

    with scope("merge"):
        for h in range(HEADS):
            rows = returned[h].astype(F32).reshape(TOK, HD).astype(BF16)
            merged[:, h * HD : (h + 1) * HD] = dot(mergehot[h], rows).astype(BF16)


def per_device(tokens, norm_gain, w_qk, w_value, w_out, send_order, place):
    vmem = pl.BlockSpec(memory_space=pltpu.VMEM)
    hbm = pl.BlockSpec(memory_space=pltpu.HBM)
    dma = pltpu.SemaphoreType.DMA
    merged = pl.pallas_call(
        kernel,
        out_shape=jax.ShapeDtypeStruct((TOK, D), BF16),
        in_specs=[hbm] * 6,
        out_specs=vmem,
        scratch_shapes=[
            pltpu.VMEM((TOK, D), BF16),
            pltpu.VMEM((1, D), F32),
            pltpu.VMEM((D, D), BF16),
            pltpu.VMEM((D, D), BF16),
            pltpu.VMEM((HEADS, TOK), I32),
            pltpu.VMEM((HEADS, TOK), I32),
            pltpu.VMEM((TOK, D), BF16),
            pltpu.VMEM((HEADS, NSX, 4, 8, 2 * HD), BF16),
            pltpu.VMEM((NDEV, 4, 8, 2 * HD), BF16),
            pltpu.VMEM((NDEV, 4, 8, HD), BF16),
            pltpu.VMEM((HEADS, NSX, 4, 8, HD), BF16),
            pltpu.VMEM((HEADS, 1, TOK), I32),
            pltpu.VMEM((NSY, 1, TOK), I32),
            pltpu.VMEM((8, TOK), I32),
            pltpu.VMEM((8, TOK, 128), I32),
            pltpu.VMEM((8, TOK, 128), I32),
            pltpu.VMEM((8, TOK), I32),
            pltpu.VMEM((HEADS, TOK, TOK), BF16),
            pltpu.VMEM((8, TOK, TOK), BF16),
            pltpu.VMEM((8, TOK, TOK), BF16),
            pltpu.VMEM((NPOS + SPAN, 2 * HD), BF16),
            pltpu.VMEM((NPOS + SPAN, HD), BF16),
            pltpu.VMEM((NPOS, HD), BF16),
            dma((6,)),
            pltpu.SemaphoreType.REGULAR,
            dma, dma, dma((2,)), dma((2,)), dma, dma, dma((2,)), dma((2,)),
        ],
        compiler_params=pltpu.CompilerParams(
            collective_id=0, has_side_effects=True, vmem_limit_bytes=VMEM_LIMIT
        ),
    )(*[
        pltpu.with_memory_space_constraint(array, pltpu.HBM)
        for array in (tokens, norm_gain.reshape(1, D), w_qk, w_value, send_order, place)
    ])
    return jnp.dot(merged, w_out, preferred_element_type=F32).astype(BF16)


def solution(mesh):
    return jax.shard_map(
        per_device,
        mesh=mesh,
        in_specs=(P(("sx", "sy"), None), P(), P(), P(), P(), P(None, ("sx", "sy")), P(None, ("sx", "sy"))),
        out_specs=P(("sx", "sy"), None),
        check_vma=False,
    )
```

time: 123 us -> 62.4 us (0.51)
  blocking collectives: 65 us -> 0 us
  Pallas kernels: 0 us -> 60.1 us
  matrix products: 21.5 us -> 2.22 us
  local copies, waits for them, and re-layouts: 15.3 us -> 0.01 us
  waiting for transfers between devices: 14.5 us -> 0 us
  other arithmetic: 5.44 us -> 0 us
    all_to_all x2 -> x0, blocking collectives: 65 us -> none  [the longest x1 41.4 us: route_out(): lax.all_to_all(buffer, ('sx', 'sy'), split_axis=1, concat_axis=1, tiled=T...]
    pallas_call x0 -> x1, Pallas kernels: none -> 60.1 us  [per_device(): pl.pallas_call(kernel, out_shape=jax.ShapeDtypeStruct((TOK, D), BF16), in...]
    dot_general x9 -> x1, matrix products: 21.5 us -> 2.22 us  [per_device(): return jnp.dot(merged, w_out, preferred_element_type=F32).astype(BF16)]
    ppermute x1 -> x0, waiting for transfers between devices: 14.5 us -> none  [shifted(): lax.ppermute(array, axis, [(i, (i + by) % peers) for i in range(peers)])]
    reshape x5 -> x0, local copies, waits for them, and re-layouts: 12.4 us -> none  [the longest x2 6.74 us: per_device(): outgoing.reshape(HEADS, devices, peer, 2 * HEAD_DIM)]
    reduce_sum x2 -> x0, other arithmetic: 2.82 us -> none  [the longest x1 1.65 us: per_device(): row_stat = jnp.mean(floats * floats, -1, keepdims=True) + 1e-06]
    all_to_all x1 -> x0, local copies, waits for them, and re-layouts: 2.16 us -> none  [route_out(): lax.all_to_all(buffer, ('sx', 'sy'), split_axis=1, concat_axis=1, tiled=T...]
    sub x1 -> x0, other arithmetic: 2 us -> none  [attend_spans(): weights = jax.nn.softmax(scores, axis=-1).astype(jnp.bfloat16)]
  transfers between devices with their start and end apart: 1 -> 0, of which waited for: 1 -> 0; matrix products, arithmetic and copies ran while one was open for 0% -> 0% of each run, Pallas kernels for 0% -> 0%
where the time goes in v2:
time: 62.4 us; the launch traced here: 62.3 us
  Pallas kernels  60.1 us (96%)
  matrix products  2.22 us (4%)
    pallas_call x1, Pallas kernels, per_device(): pl.pallas_call(kernel, out_shape=jax.ShapeDtypeStruct((TOK, D), BF16), in...  60.1 us
    dot_general x1, matrix products, per_device(): return jnp.dot(merged, w_out, preferred_element_type=F32).astype(BF16)  2.22 us

profile of v2, /device:TPU:1, one launch (start us, length us, event | category | flops | bytes accessed | tf_op | source)
XLA Modules:
  0.0 62.3 jit_solution(3587544928925921099)
XLA Ops:
  0.0 0.0 copy-start
  0.0 60.1 %shard_map.73 = bf16[512,1024]{1,0:T(8,128)(2,1)S(1)} custom-call(bf16[512,1024]{1,0:T(8,128)(2,1)} %tokens_hbm.1, f32[1,1024]{1,0:T(1,128)} %bitcast.3, bf16[1024,1024]{1,0:T(8,128)(2,1)} %wqk_hbm.1, bf16[1024,1024]{1,0:T(8,128)(2,1)} %wv_hbm.1, s32[8,512]{1,0:T(8,128)} %send_hbm.1, s32[8,512]{1,0:T(8,128)} %place_hbm.1), custom_call_target="tpu_custom_call" | custom-call | tf_op jit(solution)/shard_map/pallas_call | solution.py:335
  60.1 0.0 copy-done
  60.1 2.2 %convolution_convert_fusion = bf16[512,1024]{1,0:T(8,128)(2,1)} fusion(bf16[512,1024]{1,0:T(8,128)(2,1)S(1)} %shard_map.73, bf16[1024,1024]{1,0:T(8,128)(2,1)S(1)} %copy-done), kind=kOutput, calls=%fused_computation | convolution fusion | flops 1074266112 | bytes 4194304 | tf_op jit(solution)/shard_map/dot_general | solution.py:375
Async XLA Ops:
  0.0 60.1 %copy-start = (bf16[1024,1024]{1,0:T(8,128)(2,1)S(1)}, bf16[1024,1024]{1,0:T(8,128)(2,1)}, u32[]{:S(2)}) copy-start(bf16[1024,1024]{1,0:T(8,128)(2,1)} %param.11) | copy-start | bytes 6291460

commit v3 on v2

v3 whole, which is shorter than its diff:
```python
import random

import jax
import jax.numpy as jnp
from jax import lax
from jax.experimental import pallas as pl
from jax.experimental.pallas import tpu as pltpu
from jax.sharding import PartitionSpec as P

MESH = pl.DeviceIdType.MESH
F32, BF16, I32 = jnp.float32, jnp.bfloat16, jnp.int32
D, HEADS, HD, SPAN, TOK = 1024, 8, 128, 128, 512
NSX, NSY = 16, 8
NDEV = NSX * NSY
NPOS = 8 * TOK
TOGETHER = (15, 8, 9)
PART = 16
EACH = [[(which, part) for part in range(8)] for which in range(3)]
PLAN = [[], [], [], EACH[1], [], [], EACH[2], [], [], []]
VMEM_LIMIT = 44 * 2**20
SCALE = HD ** (-0.5)
LOG2E = 1.4426950408889634
scope = jax.named_scope


GROUPS = [(0, 0), (0, 1), (0, 3), (1, 2), (0, 2), (1, 1), (1, 3), (1, 0)]


def offsets():
    every = [
        (dx, hi, core, lo, dy)
        for dx in range(4) for hi in range(2) for core in range(2) for lo in range(2) for dy in range(4)
    ][1:]
    random.Random(1).shuffle(every)
    every.sort(key=lambda o: -(min(o[0], 4 - o[0]) + min(o[4], 4 - o[4]) + (1 if o[3] else 2 * o[1])))
    return every, [[o for o in every if (o[3], o[4]) == group] for group in GROUPS]


def reach(sx, sy):
    xs = [lax.rem(sx // 4 + d, 4) * 4 for d in range(4)]
    hi, core, lo = lax.rem(sx // 2, 2), lax.rem(sx, 2), sy // 4
    pairs = [[(1 - hi if a else hi) * 2 + (1 - core if b else core) for b in range(2)] for a in range(2)]
    txs = [[[xs[d] + pairs[a][b] for b in range(2)] for a in range(2)] for d in range(4)]
    tys = [[(1 - lo if a else lo) * 4 + lax.rem(lax.rem(sy, 4) + d, 4) for d in range(4)] for a in range(2)]
    return lambda o: (txs[o[0]][o[1]][o[2]], tys[o[3]][o[4]])


def signal(sem, target):
    pl.semaphore_signal(sem, inc=1, device_id=target, device_id_type=MESH)


def swapped(rows):
    lane = lax.broadcasted_iota(I32, rows.shape, 1)
    width = rows.shape[1]
    return jnp.where((lane // 4) % 2 == 0, pltpu.roll(rows, width - 4, 1), pltpu.roll(rows, 4, 1))


def spread(columns, out_ref):
    for j in range(8):
        out_ref[j] = jnp.broadcast_to(columns[:, j : j + 1], (TOK, 128))


def some_rows(columns, first):
    return columns.reshape(NSX, 4, 8, 8)[:, first // 8 : first // 8 + 2].reshape(TOK // 2, 8).T


def hot_rows(column):
    lane = lax.broadcasted_iota(I32, (TOK, 128), 1)
    return jnp.concatenate(
        [jnp.where(column == lane + 128 * c, 1.0, 0.0).astype(BF16) for c in range(TOK // 128)], axis=1
    )


def hot_columns(row):
    token = lax.broadcasted_iota(I32, (TOK, row.shape[1]), 0)
    return jnp.where(token == row, 1.0, 0.0).astype(BF16)


def dot(a, b):
    return jnp.dot(a, b, preferred_element_type=F32)


def halves(first, second):
    low = lax.broadcasted_iota(I32, first.shape, 1) < 4
    return jnp.where(low, first, second)


def kernel(
    tokens_hbm, gain_hbm, wqk_hbm, wv_hbm, send_hbm, place_hbm, merged,
    tokens, gain, weights, send_ref, place_ref, normed, outgoing, arrived, leaving, returned, placeout, placein, placerow,
    placecol, turned, both, sendrow, mergehot, orderhot, leavehot, ordered, unit, sorted_out,
    partial, load_sem, weight_sem, met_sem, place_s, place_r, out_s, out_r, halo_s, halo_r, back_s, back_r,
):
    sx, sy = lax.axis_index("sx"), lax.axis_index("sy")
    me = sx * NSY + sy
    at_offset = reach(sx, sy)
    every, groups = offsets()
    heads = [at_offset((0, 0, 0, *group))[1] for group in GROUPS]

    with scope("signal"):
        barrier = pltpu.get_barrier_semaphore()
        for k in range(1, NSX):
            signal(barrier, (lax.rem(sx + k, NSX), sy))
        for k in range(1, NSY):
            signal(barrier, (sx, lax.rem(sy + k, NSY)))
        loads = [
            pltpu.make_async_copy(src, dst, load_sem.at[n])
            for n, (src, dst) in enumerate([
                (send_hbm, send_ref), (place_hbm, place_ref), (gain_hbm, gain), (tokens_hbm, tokens),
            ])
        ]
        for load in loads:
            load.start()
        weight_loads = []
        for n, h in enumerate(heads):
            columns = pl.ds(pl.multiple_of(h * HD, HD), HD)
            weight_loads.append([
                pltpu.make_async_copy(src.at[:, columns], weights.at[n, :, pl.ds(at, HD)], weight_sem.at[n, at // HD])
                for src, at in ((wqk_hbm, 0), (wv_hbm, HD))
            ])
        for load in weight_loads[0]:
            load.start()

    with scope("index"):
        loads[0].wait()
        for pair in weight_loads[1:]:
            for load in pair:
                load.start()
        for n, h in enumerate(heads):
            turned[n : n + 1, :] = send_ref[pl.ds(h, 1), :]
        odd = lax.rem(sy, 2) == 1
        rows = turned[...]
        columns = jnp.where(odd, swapped(rows), rows).T

    with scope("norm"):
        loads[2].wait()
        loads[3].wait()

        def norm(i, _):
            at = pl.ds(pl.multiple_of(i * 128, 128), 128)
            rows = tokens[at, :].astype(F32)
            stat = jnp.mean(rows * rows, -1, keepdims=True) + 1e-06
            normed[at, :] = (rows * lax.rsqrt(stat) * gain[...]).astype(BF16)
            return 0

        lax.fori_loop(0, TOK // 128, norm, 0)

    def project(n):
        for load in weight_loads[n]:
            load.wait()
        both[n % 2] = dot(normed[...], weights[n]).astype(BF16)

    def permute(n):
        rows = dot(hot_rows(jnp.broadcast_to(columns[:, n : n + 1], (TOK, 128))), both[n % 2])
        outgoing[heads[n]] = rows.reshape(NSX, 4, 8, 2 * HD).astype(BF16)

    def send_rows(first, count, sem, target, sent):
        tx, ty = target
        pltpu.make_async_remote_copy(
            outgoing.at[ty, tx, pl.ds(first, count)],
            arrived.at[me, pl.ds(first, count)],
            out_s.at[sent],
            out_r.at[sem],
            device_id=target,
            device_id_type=MESH,
        ).start()

    with scope("project0"):
        project(0)

    with scope("permute0"):
        project(1)
        permute(0)

    with scope("barrier1"):
        loads[1].wait()
        for h in range(HEADS):
            placeout[h] = place_ref[h : h + 1, :]
        pl.semaphore_wait(barrier, NSX - 1 + NSY - 1)
        for k in range(1, NSY):
            signal(met_sem, (sx, lax.rem(sy + k, NSY)))

    with scope("send_near"):
        for o in groups[0]:
            send_rows(2, 2, 0, at_offset(o), 0)
        for k in range(1, NSY):
            ty = lax.rem(sy + k, NSY)
            pltpu.make_async_remote_copy(
                placeout.at[ty], placein.at[sy], place_s, place_r, device_id=(sx, ty), device_id_type=MESH
            ).start()

    for n in range(1, 8):
        with scope(f"project{n}"):
            if n < 7:
                project(n + 1)
            permute(n)
            if n == 1:
                pl.semaphore_wait(met_sem, NSY - 1)
            for o in groups[n]:
                send_rows(2, 2, 0, at_offset(o), n)

    arrived[me] = outgoing[sy, sx]

    with scope("tables"):
        rows = send_ref[...]
        columns = jnp.where(odd, swapped(rows), rows).T
        for part in range(2):
            sendrow[part] = some_rows(columns, 16 * part)
        def table(h, _):
            for part in range(2):
                mergehot[part, h] = hot_columns(sendrow[part, pl.ds(h, 1), :])
            return 0

        lax.fori_loop(0, HEADS, table, 0)
        whole_place = pltpu.make_async_remote_copy(
            placein.at[pl.ds(0, NSY - 1)], placein.at[pl.ds(0, NSY - 1)], place_s, place_r, device_id=(sx, sy),
            device_id_type=MESH,
        )
        whole_place.wait_send()
        whole_place.wait_recv()
        placein[sy] = placeout[sy]
        for j in range(8):
            placerow[j : j + 1, :] = placein[j]
        block = lax.broadcasted_iota(I32, (8, TOK), 0)
        placerow[...] = jnp.where(block % 2 == 1, swapped(placerow[...]), placerow[...])
        spread(placerow[...].T, placecol)

        def place_table(j, _):
            orderhot[j] = hot_columns(placerow[pl.ds(j, 1), :])
            leavehot[j] = hot_rows(placecol[j])
            return 0

        lax.fori_loop(0, 8, place_table, 0)

    def whole(ref, send_sem, recv_sem):
        return pltpu.make_async_remote_copy(
            ref, ref, send_sem, recv_sem, device_id=(sx, sy), device_id_type=MESH
        )

    def units(keys, at):
        stat = jnp.sum(keys * keys, -1, keepdims=True) + 1e-06
        unit[at, :] = (keys * lax.rsqrt(stat)).astype(BF16)

    def order(q):
        group = arrived[:, q].astype(F32).reshape(NDEV // 2, 2, 8, 2 * HD)
        even, odd = group[:, 0], group[:, 1]
        for b, pair in ((1, (odd, even)), (0, (even, odd))):
            j = 2 * q + b
            mixed = halves(*pair).reshape(TOK, 2 * HD).astype(BF16)
            at = pl.ds(SPAN + j * TOK, TOK)
            rows = dot(orderhot[j], mixed)
            ordered[at, :] = rows.astype(BF16)
            units(rows[:, :HD], at)

    def attend(first, count, together):
        diagonal = lax.broadcasted_iota(I32, (SPAN, SPAN), 0) == lax.broadcasted_iota(I32, (SPAN, SPAN), 1)

        def some(g, _):
            for u in range(together):
                c = first + g * together + u
                at = pl.ds(pl.multiple_of(c * SPAN, SPAN), 2 * SPAN)
                query = ordered[pl.ds(pl.multiple_of(c * SPAN + SPAN, SPAN), SPAN), :HD]
                scores = lax.dot_general(query, unit[at, :], (((1,), (1,)), ((), ())), preferred_element_type=F32)
                before, own = scores[:, :SPAN], jnp.where(diagonal, -100000.0 / SCALE, scores[:, SPAN:])
                peak = jnp.max(jnp.maximum(before, own), -1, keepdims=True)
                before, own = jnp.exp2((before - peak) * (SCALE * LOG2E)), jnp.exp2((own - peak) * (SCALE * LOG2E))
                share = 1.0 / jnp.sum(before + own, -1, keepdims=True)
                shares = jnp.concatenate([before * share, own * share], axis=1).astype(BF16)
                sorted_out[pl.ds(pl.multiple_of(c * SPAN, SPAN), SPAN), :] = dot(shares, ordered[at, HD:]).astype(BF16)
            return 0

        lax.fori_loop(0, count // together, some, 0)

    def leave(q):
        parts = []
        for b in range(2):
            j = q * 2 + b
            rows = sorted_out[pl.ds(j * TOK, TOK), :]
            parts.append(dot(leavehot[j], rows).reshape(NDEV // 2, 8, HD))
        pair = jnp.stack([halves(parts[0], parts[1]), halves(parts[1], parts[0])], axis=1)
        leaving[:, q] = pair.reshape(NDEV, 8, HD).astype(BF16)

    def send_back(first, count, target, sem):
        tx, ty = target
        pltpu.make_async_remote_copy(
            leaving.at[tx * NSY + ty, pl.ds(first, count)],
            returned.at[sy, sx, pl.ds(first, count)],
            back_s.at[sem],
            back_r.at[sem],
            device_id=target,
            device_id_type=MESH,
        ).start()

    def came(first, count, sem):
        whole(arrived.at[pl.ds(0, NDEV - 1), pl.ds(first, count)], out_s.at[0], out_r.at[sem]).wait_recv()

    def left(n, count, messages):
        whole(arrived.at[pl.ds(0, messages), pl.ds(0, count)], out_s.at[n], out_r.at[0]).wait_send()

    def parts_of(n):
        return every[n * PART : (n + 1) * PART]

    def send_part(which, n):
        for o in parts_of(n):
            send_rows(2 - which, 1, which, at_offset(o), 8 * which + n)

    with scope("send_out1"):
        for n in range(8):
            left(n, 2, len(groups[n]))
            for which, part in PLAN[n]:
                send_part(which, part)

    with scope("wait_out0"):
        came(2, 2, 0)

    with scope("order0"):
        order(3)
        halo = pltpu.make_async_remote_copy(
            ordered.at[pl.ds(NPOS, SPAN)], ordered.at[pl.ds(0, SPAN)], halo_s, halo_r,
            device_id=(lax.rem(sx + 1, NSX), sy), device_id_type=MESH,
        )
        halo.start()
        order(2)

    with scope("attend0"):
        for which, part in PLAN[8]:
            send_part(which, part)
        attend(17, 15, TOGETHER[0])
        for which, part in PLAN[9]:
            send_part(which, part)

    with scope("leave0"):
        leave(3)

    with scope("back0"):
        for o in every:
            send_back(3, 1, at_offset(o), 0)

    with scope("wait_out1"):
        came(1, 1, 1)

    with scope("order1"):
        order(1)

    with scope("attend1"):
        attend(9, 8, TOGETHER[1])

    with scope("leave1"):
        leave(2)

    with scope("back1"):
        for o in every:
            send_back(2, 1, at_offset(o), 1)

    with scope("wait_out2"):
        came(0, 1, 2)
        for n in range(8, 24):
            left(n, 1, len(parts_of(n % 8)))

    with scope("order2"):
        order(0)
        halo.wait_send()
        halo.wait_recv()
        units(ordered[pl.ds(0, SPAN), :HD].astype(F32), pl.ds(0, SPAN))

    with scope("attend2"):
        attend(0, 9, TOGETHER[2])

    with scope("leave2"):
        leave(1)
        leave(0)

    with scope("back2"):
        for o in every:
            send_back(0, 2, at_offset(o), 2)
        returned[sy, sx] = leaving[me]

    def merge(part, h):
        rows = returned[h, :, pl.ds(2 * part, 2)].astype(F32).reshape(TOK // 2, HD).astype(BF16)
        return dot(mergehot[part, h], rows)

    with scope("wait_back0"):
        for n in range(2):
            back = whole(leaving.at[pl.ds(0, NDEV - 1), pl.ds(0, 1)], back_s.at[n], back_r.at[n])
            back.wait_send()
            back.wait_recv()

    with scope("merge0"):
        for h in range(HEADS):
            partial[h] = merge(1, h)

    with scope("wait_back2"):
        back = whole(leaving.at[pl.ds(0, NDEV - 1), pl.ds(0, 2)], back_s.at[2], back_r.at[2])
        back.wait_send()
        back.wait_recv()

    with scope("merge"):
        for h in range(HEADS):
            merged[:, h * HD : (h + 1) * HD] = (partial[h] + merge(0, h)).astype(BF16)


def per_device(tokens, norm_gain, w_qk, w_value, w_out, send_order, place):
    vmem = pl.BlockSpec(memory_space=pltpu.VMEM)
    hbm = pl.BlockSpec(memory_space=pltpu.HBM)
    dma = pltpu.SemaphoreType.DMA
    merged = pl.pallas_call(
        kernel,
        out_shape=jax.ShapeDtypeStruct((TOK, D), BF16),
        in_specs=[hbm] * 6,
        out_specs=vmem,
        scratch_shapes=[
            pltpu.VMEM((TOK, D), BF16),
            pltpu.VMEM((1, D), F32),
            pltpu.VMEM((HEADS, D, 2 * HD), BF16),
            pltpu.VMEM((HEADS, TOK), I32),
            pltpu.VMEM((HEADS, TOK), I32),
            pltpu.VMEM((TOK, D), BF16),
            pltpu.VMEM((HEADS, NSX, 4, 8, 2 * HD), BF16),
            pltpu.VMEM((NDEV, 4, 8, 2 * HD), BF16),
            pltpu.VMEM((NDEV, 4, 8, HD), BF16),
            pltpu.VMEM((HEADS, NSX, 4, 8, HD), BF16),
            pltpu.VMEM((HEADS, 1, TOK), I32),
            pltpu.VMEM((NSY, 1, TOK), I32),
            pltpu.VMEM((8, TOK), I32),
            pltpu.VMEM((8, TOK, 128), I32),
            pltpu.VMEM((8, TOK), I32),
            pltpu.VMEM((2, TOK, 2 * HD), BF16),
            pltpu.VMEM((2, 8, TOK // 2), I32),
            pltpu.VMEM((2, HEADS, TOK, TOK // 2), BF16),
            pltpu.VMEM((8, TOK, TOK), BF16),
            pltpu.VMEM((8, TOK, TOK), BF16),
            pltpu.VMEM((NPOS + SPAN, 2 * HD), BF16),
            pltpu.VMEM((NPOS + SPAN, HD), BF16),
            pltpu.VMEM((NPOS, HD), BF16),
            pltpu.VMEM((HEADS, TOK, HD), F32),
            dma((4,)),
            dma((HEADS, 2)),
            pltpu.SemaphoreType.REGULAR,
            dma, dma, dma((24,)), dma((3,)), dma, dma, dma((3,)), dma((3,)),
        ],
        compiler_params=pltpu.CompilerParams(
            collective_id=0, has_side_effects=True, vmem_limit_bytes=VMEM_LIMIT
        ),
    )(*[
        pltpu.with_memory_space_constraint(array, pltpu.HBM)
        for array in (tokens, norm_gain.reshape(1, D), w_qk, w_value, send_order, place)
    ])
    return jnp.dot(merged, w_out, preferred_element_type=F32).astype(BF16)


def solution(mesh):
    return jax.shard_map(
        per_device,
        mesh=mesh,
        in_specs=(P(("sx", "sy"), None), P(), P(), P(), P(), P(None, ("sx", "sy")), P(None, ("sx", "sy"))),
        out_specs=P(("sx", "sy"), None),
        check_vma=False,
    )
```

time: 62.4 us -> 56.5 us (0.905)
  Pallas kernels: 60.1 us -> 54.1 us
    pallas_call x1, Pallas kernels: 60.1 us -> 54.1 us  [per_device(): pl.pallas_call(kernel, out_shape=jax.ShapeDtypeStruct((TOK, D), BF16), in...]
where the time goes in v3:
time: 56.5 us; the launch traced here: 56.4 us
  Pallas kernels  54.1 us (96%)
  matrix products  2.22 us (4%)
    pallas_call x1, Pallas kernels, per_device(): pl.pallas_call(kernel, out_shape=jax.ShapeDtypeStruct((TOK, D), BF16), in...  54.1 us
    dot_general x1, matrix products, per_device(): return jnp.dot(merged, w_out, preferred_element_type=F32).astype(BF16)  2.22 us

profile of v3, /device:TPU:1, one launch (start us, length us, event | category | flops | bytes accessed | tf_op | source)
XLA Modules:
  0.0 56.4 jit_solution(14397602740938110874)
XLA Ops:
  0.0 0.0 copy-start
  0.0 54.1 %shard_map.73 = bf16[512,1024]{1,0:T(8,128)(2,1)S(1)} custom-call(bf16[512,1024]{1,0:T(8,128)(2,1)} %tokens_hbm.1, f32[1,1024]{1,0:T(1,128)} %bitcast.3, bf16[1024,1024]{1,0:T(8,128)(2,1)} %wqk_hbm.1, bf16[1024,1024]{1,0:T(8,128)(2,1)} %wv_hbm.1, s32[8,512]{1,0:T(8,128)} %send_hbm.1, s32[8,512]{1,0:T(8,128)} %place_hbm.1), custom_call_target="tpu_custom_call" | custom-call | tf_op jit(solution)/shard_map/pallas_call | solution.py:406
  54.2 0.0 copy-done
  54.2 2.2 %convolution_convert_fusion = bf16[512,1024]{1,0:T(8,128)(2,1)} fusion(bf16[512,1024]{1,0:T(8,128)(2,1)S(1)} %shard_map.73, bf16[1024,1024]{1,0:T(8,128)(2,1)S(1)} %copy-done), kind=kOutput, calls=%fused_computation | convolution fusion | flops 1074266112 | bytes 4194304 | tf_op jit(solution)/shard_map/dot_general | solution.py:448
Async XLA Ops:
  0.0 54.2 %copy-start = (bf16[1024,1024]{1,0:T(8,128)(2,1)S(1)}, bf16[1024,1024]{1,0:T(8,128)(2,1)}, u32[]{:S(2)}) copy-start(bf16[1024,1024]{1,0:T(8,128)(2,1)} %param.11) | copy-start | bytes 6291460

commit v4 on v3

--- a/solution.py
+++ b/solution.py
@@ -13,10 +13,7 @@
 NSX, NSY = 16, 8
 NDEV = NSX * NSY
 NPOS = 8 * TOK
-TOGETHER = (15, 8, 9)
-PART = 16
-EACH = [[(which, part) for part in range(8)] for which in range(3)]
-PLAN = [[], [], [], EACH[1], [], [], EACH[2], [], [], []]
+BATCHES = [(1, 2), (3, 4), (5, 6, 7)]
 VMEM_LIMIT = 44 * 2**20
 SCALE = HD ** (-0.5)
 LOG2E = 1.4426950408889634
@@ -60,8 +57,8 @@
         out_ref[j] = jnp.broadcast_to(columns[:, j : j + 1], (TOK, 128))
 
 
-def some_rows(columns, first):
-    return columns.reshape(NSX, 4, 8, 8)[:, first // 8 : first // 8 + 2].reshape(TOK // 2, 8).T
+def some_rows(columns, q):
+    return columns.reshape(NSX, 4, 8, 8)[:, q].reshape(TOK // 4, 8).T
 
 
 def hot_rows(column):
@@ -106,7 +103,8 @@
         loads = [
             pltpu.make_async_copy(src, dst, load_sem.at[n])
             for n, (src, dst) in enumerate([
-                (send_hbm, send_ref), (place_hbm, place_ref), (gain_hbm, gain), (tokens_hbm, tokens),
+                (send_hbm, send_ref), (place_hbm, place_ref), (gain_hbm, gain),
+                *[(tokens_hbm.at[pl.ds(i, 128)], tokens.at[pl.ds(i, 128)]) for i in range(0, TOK, 128)],
             ])
         ]
         for load in loads:
@@ -134,16 +132,11 @@
 
     with scope("norm"):
         loads[2].wait()
-        loads[3].wait()
-
-        def norm(i, _):
-            at = pl.ds(pl.multiple_of(i * 128, 128), 128)
-            rows = tokens[at, :].astype(F32)
+        for i in range(4):
+            loads[3 + i].wait()
+            rows = tokens[128 * i : 128 * i + 128, :].astype(F32)
             stat = jnp.mean(rows * rows, -1, keepdims=True) + 1e-06
-            normed[at, :] = (rows * lax.rsqrt(stat) * gain[...]).astype(BF16)
-            return 0
-
-        lax.fori_loop(0, TOK // 128, norm, 0)
+            normed[128 * i : 128 * i + 128, :] = (rows * lax.rsqrt(stat) * gain[...]).astype(BF16)
 
     def project(n):
         for load in weight_loads[n]:
@@ -154,13 +147,13 @@
         rows = dot(hot_rows(jnp.broadcast_to(columns[:, n : n + 1], (TOK, 128))), both[n % 2])
         outgoing[heads[n]] = rows.reshape(NSX, 4, 8, 2 * HD).astype(BF16)
 
-    def send_rows(first, count, sem, target, sent):
+    def send_rows(first, count, which, target):
         tx, ty = target
         pltpu.make_async_remote_copy(
             outgoing.at[ty, tx, pl.ds(first, count)],
             arrived.at[me, pl.ds(first, count)],
-            out_s.at[sent],
-            out_r.at[sem],
+            out_s.at[which],
+            out_r.at[which],
             device_id=target,
             device_id_type=MESH,
         ).start()
@@ -182,33 +175,52 @@
 
     with scope("send_near"):
         for o in groups[0]:
-            send_rows(2, 2, 0, at_offset(o), 0)
+            send_rows(2, 2, 0, at_offset(o))
         for k in range(1, NSY):
             ty = lax.rem(sy + k, NSY)
             pltpu.make_async_remote_copy(
                 placeout.at[ty], placein.at[sy], place_s, place_r, device_id=(sx, ty), device_id_type=MESH
             ).start()
 
-    for n in range(1, 8):
-        with scope(f"project{n}"):
-            if n < 7:
-                project(n + 1)
-            permute(n)
-            if n == 1:
+    for batch in BATCHES:
+        with scope(f"project{batch[0]}"):
+            for n in batch:
+                if n < 7:
+                    project(n + 1)
+                permute(n)
+        with scope(f"send{batch[0]}"):
+            if batch[0] == 1:
                 pl.semaphore_wait(met_sem, NSY - 1)
-            for o in groups[n]:
-                send_rows(2, 2, 0, at_offset(o), n)
+            for o in every:
+                n = GROUPS.index(o[3:])
+                if n in batch:
+                    send_rows(2, 2, 0, at_offset(o))
 
     arrived[me] = outgoing[sy, sx]
+
+    def whole(ref, send_sem, recv_sem):
+        return pltpu.make_async_remote_copy(
+            ref, ref, send_sem, recv_sem, device_id=(sx, sy), device_id_type=MESH
+        )
+
+    with scope("send_rest"):
+        for which in (1, 2):
+            for o in every:
+                send_rows(2 - which, 1, which, at_offset(o))
+
+    def came(which):
+        out = whole(arrived.at[pl.ds(0, NDEV - 1), pl.ds(0, (2, 1, 1)[which])], out_s.at[which], out_r.at[which])
+        out.wait_send()
+        out.wait_recv()
 
     with scope("tables"):
         rows = send_ref[...]
         columns = jnp.where(odd, swapped(rows), rows).T
-        for part in range(2):
-            sendrow[part] = some_rows(columns, 16 * part)
+        for q in range(4):
+            sendrow[q] = some_rows(columns, q)
         def table(h, _):
-            for part in range(2):
-                mergehot[part, h] = hot_columns(sendrow[part, pl.ds(h, 1), :])
+            for q in range(4):
+                mergehot[q, h] = hot_columns(sendrow[q, pl.ds(h, 1), :])
             return 0
 
         lax.fori_loop(0, HEADS, table, 0)
@@ -232,44 +244,32 @@
 
         lax.fori_loop(0, 8, place_table, 0)
 
-    def whole(ref, send_sem, recv_sem):
-        return pltpu.make_async_remote_copy(
-            ref, ref, send_sem, recv_sem, device_id=(sx, sy), device_id_type=MESH
-        )
-
     def units(keys, at):
         stat = jnp.sum(keys * keys, -1, keepdims=True) + 1e-06
         unit[at, :] = (keys * lax.rsqrt(stat)).astype(BF16)
 
-    def order(q):
+    def order(q, b):
         group = arrived[:, q].astype(F32).reshape(NDEV // 2, 2, 8, 2 * HD)
         even, odd = group[:, 0], group[:, 1]
-        for b, pair in ((1, (odd, even)), (0, (even, odd))):
-            j = 2 * q + b
-            mixed = halves(*pair).reshape(TOK, 2 * HD).astype(BF16)
-            at = pl.ds(SPAN + j * TOK, TOK)
-            rows = dot(orderhot[j], mixed)
-            ordered[at, :] = rows.astype(BF16)
-            units(rows[:, :HD], at)
-
-    def attend(first, count, together):
+        j = 2 * q + b
+        mixed = (halves(odd, even) if b else halves(even, odd)).reshape(TOK, 2 * HD).astype(BF16)
+        at = pl.ds(SPAN + j * TOK, TOK)
+        rows = dot(orderhot[j], mixed)
+        ordered[at, :] = rows.astype(BF16)
+        units(rows[:, :HD], at)
+
+    def attend(first, count):
         diagonal = lax.broadcasted_iota(I32, (SPAN, SPAN), 0) == lax.broadcasted_iota(I32, (SPAN, SPAN), 1)
-
-        def some(g, _):
-            for u in range(together):
-                c = first + g * together + u
-                at = pl.ds(pl.multiple_of(c * SPAN, SPAN), 2 * SPAN)
-                query = ordered[pl.ds(pl.multiple_of(c * SPAN + SPAN, SPAN), SPAN), :HD]
-                scores = lax.dot_general(query, unit[at, :], (((1,), (1,)), ((), ())), preferred_element_type=F32)
-                before, own = scores[:, :SPAN], jnp.where(diagonal, -100000.0 / SCALE, scores[:, SPAN:])
-                peak = jnp.max(jnp.maximum(before, own), -1, keepdims=True)
-                before, own = jnp.exp2((before - peak) * (SCALE * LOG2E)), jnp.exp2((own - peak) * (SCALE * LOG2E))
-                share = 1.0 / jnp.sum(before + own, -1, keepdims=True)
-                shares = jnp.concatenate([before * share, own * share], axis=1).astype(BF16)
-                sorted_out[pl.ds(pl.multiple_of(c * SPAN, SPAN), SPAN), :] = dot(shares, ordered[at, HD:]).astype(BF16)
-            return 0
-
-        lax.fori_loop(0, count // together, some, 0)
+        for c in range(first, first + count):
+            at = pl.ds(c * SPAN, 2 * SPAN)
+            query = ordered[pl.ds(c * SPAN + SPAN, SPAN), :HD]
+            scores = lax.dot_general(query, unit[at, :], (((1,), (1,)), ((), ())), preferred_element_type=F32)
+            before, own = scores[:, :SPAN], jnp.where(diagonal, -100000.0 / SCALE, scores[:, SPAN:])
+            peak = jnp.max(jnp.maximum(before, own), -1, keepdims=True)
+            before, own = jnp.exp2((before - peak) * (SCALE * LOG2E)), jnp.exp2((own - peak) * (SCALE * LOG2E))
+            share = 1.0 / jnp.sum(before + own, -1, keepdims=True)
+            shares = jnp.concatenate([before * share, own * share], axis=1).astype(BF16)
+            sorted_out[pl.ds(c * SPAN, SPAN), :] = dot(shares, ordered[at, HD:]).astype(BF16)
 
     def leave(q):
         parts = []
@@ -280,119 +280,106 @@
         pair = jnp.stack([halves(parts[0], parts[1]), halves(parts[1], parts[0])], axis=1)
         leaving[:, q] = pair.reshape(NDEV, 8, HD).astype(BF16)
 
-    def send_back(first, count, target, sem):
-        tx, ty = target
-        pltpu.make_async_remote_copy(
-            leaving.at[tx * NSY + ty, pl.ds(first, count)],
-            returned.at[sy, sx, pl.ds(first, count)],
-            back_s.at[sem],
-            back_r.at[sem],
-            device_id=target,
-            device_id_type=MESH,
-        ).start()
-
-    def came(first, count, sem):
-        whole(arrived.at[pl.ds(0, NDEV - 1), pl.ds(first, count)], out_s.at[0], out_r.at[sem]).wait_recv()
-
-    def left(n, count, messages):
-        whole(arrived.at[pl.ds(0, messages), pl.ds(0, count)], out_s.at[n], out_r.at[0]).wait_send()
-
-    def parts_of(n):
-        return every[n * PART : (n + 1) * PART]
-
-    def send_part(which, n):
-        for o in parts_of(n):
-            send_rows(2 - which, 1, which, at_offset(o), 8 * which + n)
-
-    with scope("send_out1"):
-        for n in range(8):
-            left(n, 2, len(groups[n]))
-            for which, part in PLAN[n]:
-                send_part(which, part)
+    def send_back(q):
+        for o in every:
+            tx, ty = at_offset(o)
+            pltpu.make_async_remote_copy(
+                leaving.at[tx * NSY + ty, q],
+                returned.at[sy, sx, q],
+                back_s.at[q],
+                back_r.at[q],
+                device_id=(tx, ty),
+                device_id_type=MESH,
+            ).start()
+        returned[sy, sx, q] = leaving[me, q]
+
+    def returns(q):
+        back = whole(leaving.at[pl.ds(0, NDEV - 1), 0], back_s.at[q], back_r.at[q])
+        back.wait_send()
+        back.wait_recv()
+
+    def merge(q, h):
+        rows = returned[h, :, q].astype(F32).reshape(TOK // 4, HD).astype(BF16)
+        return dot(mergehot[q, h], rows)
 
     with scope("wait_out0"):
-        came(2, 2, 0)
+        came(0)
 
     with scope("order0"):
-        order(3)
+        order(3, 1)
+        order(3, 0)
         halo = pltpu.make_async_remote_copy(
             ordered.at[pl.ds(NPOS, SPAN)], ordered.at[pl.ds(0, SPAN)], halo_s, halo_r,
             device_id=(lax.rem(sx + 1, NSX), sy), device_id_type=MESH,
         )
         halo.start()
-        order(2)
+        order(2, 1)
+        order(2, 0)
 
     with scope("attend0"):
-        for which, part in PLAN[8]:
-            send_part(which, part)
-        attend(17, 15, TOGETHER[0])
-        for which, part in PLAN[9]:
-            send_part(which, part)
+        attend(17, 15)
 
     with scope("leave0"):
         leave(3)
 
     with scope("back0"):
-        for o in every:
-            send_back(3, 1, at_offset(o), 0)
+        send_back(3)
 
     with scope("wait_out1"):
-        came(1, 1, 1)
+        came(1)
 
     with scope("order1"):
-        order(1)
+        order(1, 1)
+        order(1, 0)
 
     with scope("attend1"):
-        attend(9, 8, TOGETHER[1])
+        attend(9, 8)
 
     with scope("leave1"):
         leave(2)
 
     with scope("back1"):
-        for o in every:
-            send_back(2, 1, at_offset(o), 1)
+        send_back(2)
 
     with scope("wait_out2"):
-        came(0, 1, 2)
-        for n in range(8, 24):
-            left(n, 1, len(parts_of(n % 8)))
+        came(2)
 
     with scope("order2"):
-        order(0)
+        order(0, 1)
+
+    with scope("attend2"):
+        attend(8, 1)
+
+    with scope("leave2"):
+        leave(1)
+
+    with scope("back2"):
+        send_back(1)
+
+    with scope("order3"):
+        order(0, 0)
         halo.wait_send()
         halo.wait_recv()
         units(ordered[pl.ds(0, SPAN), :HD].astype(F32), pl.ds(0, SPAN))
 
-    with scope("attend2"):
-        attend(0, 9, TOGETHER[2])
-
-    with scope("leave2"):
-        leave(1)
+    with scope("attend3"):
+        attend(0, 8)
+
+    with scope("leave3"):
         leave(0)
 
-    with scope("back2"):
-        for o in every:
-            send_back(0, 2, at_offset(o), 2)
-        returned[sy, sx] = leaving[me]
-
-    def merge(part, h):
-        rows = returned[h, :, pl.ds(2 * part, 2)].astype(F32).reshape(TOK // 2, HD).astype(BF16)
-        return dot(mergehot[part, h], rows)
+    with scope("back3"):
+        send_back(0)
+
+    for q in (3, 2, 1):
+        with scope(f"wait_back{q}"):
+            returns(q)
+        with scope(f"merge{q}"):
+            for h in range(HEADS):
+                partial[h] = merge(q, h) if q == 3 else partial[h] + merge(q, h)
 
     with scope("wait_back0"):
-        for n in range(2):
-            back = whole(leaving.at[pl.ds(0, NDEV - 1), pl.ds(0, 1)], back_s.at[n], back_r.at[n])
-            back.wait_send()
-            back.wait_recv()
-
-    with scope("merge0"):
-        for h in range(HEADS):
-            partial[h] = merge(1, h)
-
-    with scope("wait_back2"):
-        back = whole(leaving.at[pl.ds(0, NDEV - 1), pl.ds(0, 2)], back_s.at[2], back_r.at[2])
-        back.wait_send()
-        back.wait_recv()
+        returns(0)
 
     with scope("merge"):
         for h in range(HEADS):
@@ -425,18 +412,18 @@
             pltpu.VMEM((8, TOK, 128), I32),
             pltpu.VMEM((8, TOK), I32),
             pltpu.VMEM((2, TOK, 2 * HD), BF16),
-            pltpu.VMEM((2, 8, TOK // 2), I32),
-            pltpu.VMEM((2, HEADS, TOK, TOK // 2), BF16),
+            pltpu.VMEM((4, 8, TOK // 4), I32),
+            pltpu.VMEM((4, HEADS, TOK, TOK // 4), BF16),
             pltpu.VMEM((8, TOK, TOK), BF16),
             pltpu.VMEM((8, TOK, TOK), BF16),
             pltpu.VMEM((NPOS + SPAN, 2 * HD), BF16),
             pltpu.VMEM((NPOS + SPAN, HD), BF16),
             pltpu.VMEM((NPOS, HD), BF16),
             pltpu.VMEM((HEADS, TOK, HD), F32),
-            dma((4,)),
+            dma((7,)),
             dma((HEADS, 2)),
             pltpu.SemaphoreType.REGULAR,
-            dma, dma, dma((24,)), dma((3,)), dma, dma, dma((3,)), dma((3,)),
+            dma, dma, dma((3,)), dma((3,)), dma, dma, dma((4,)), dma((4,)),
         ],
         compiler_params=pltpu.CompilerParams(
             collective_id=0, has_side_effects=True, vmem_limit_bytes=VMEM_LIMIT

time: 56.5 us -> 52.7 us (0.933)
  Pallas kernels: 54.1 us -> 50.3 us
    pallas_call x1, Pallas kernels: 54.1 us -> 50.3 us  [per_device(): pl.pallas_call(kernel, out_shape=jax.ShapeDtypeStruct((TOK, D), BF16), in...]
where the time goes in v4:
time: 52.7 us; the launch traced here: 52.6 us
  Pallas kernels  50.3 us (95%)
  matrix products  2.22 us (4%)
    pallas_call x1, Pallas kernels, per_device(): pl.pallas_call(kernel, out_shape=jax.ShapeDtypeStruct((TOK, D), BF16), in...  50.3 us
    dot_general x1, matrix products, per_device(): return jnp.dot(merged, w_out, preferred_element_type=F32).astype(BF16)  2.22 us

profile of v4, /device:TPU:1, one launch (start us, length us, event | category | flops | bytes accessed | tf_op | source)
XLA Modules:
  0.0 52.6 jit_solution(7048060290100985574)
XLA Ops:
  0.0 0.0 copy-start
  0.0 50.3 %shard_map.73 = bf16[512,1024]{1,0:T(8,128)(2,1)S(1)} custom-call(bf16[512,1024]{1,0:T(8,128)(2,1)} %tokens_hbm.1, f32[1,1024]{1,0:T(1,128)} %bitcast.3, bf16[1024,1024]{1,0:T(8,128)(2,1)} %wqk_hbm.1, bf16[1024,1024]{1,0:T(8,128)(2,1)} %wv_hbm.1, s32[8,512]{1,0:T(8,128)} %send_hbm.1, s32[8,512]{1,0:T(8,128)} %place_hbm.1), custom_call_target="tpu_custom_call" | custom-call | tf_op jit(solution)/shard_map/pallas_call | solution.py:393
  50.3 0.0 copy-done
  50.4 2.2 %convolution_convert_fusion = bf16[512,1024]{1,0:T(8,128)(2,1)} fusion(bf16[512,1024]{1,0:T(8,128)(2,1)S(1)} %shard_map.73, bf16[1024,1024]{1,0:T(8,128)(2,1)S(1)} %copy-done), kind=kOutput, calls=%fused_computation | convolution fusion | flops 1074266112 | bytes 4194304 | tf_op jit(solution)/shard_map/dot_general | solution.py:435
Async XLA Ops:
  0.0 50.3 %copy-start = (bf16[1024,1024]{1,0:T(8,128)(2,1)S(1)}, bf16[1024,1024]{1,0:T(8,128)(2,1)}, u32[]{:S(2)}) copy-start(bf16[1024,1024]{1,0:T(8,128)(2,1)} %param.11) | copy-start | bytes 6291460

commit v5 on v4

--- a/solution.py
+++ b/solution.py
@@ -249,7 +249,7 @@
         unit[at, :] = (keys * lax.rsqrt(stat)).astype(BF16)
 
     def order(q, b):
-        group = arrived[:, q].astype(F32).reshape(NDEV // 2, 2, 8, 2 * HD)
+        group = arrived[pl.ds(0, NDEV), q].astype(F32).reshape(NDEV // 2, 2, 8, 2 * HD)
         even, odd = group[:, 0], group[:, 1]
         j = 2 * q + b
         mixed = (halves(odd, even) if b else halves(even, odd)).reshape(TOK, 2 * HD).astype(BF16)
@@ -278,7 +278,7 @@
             rows = sorted_out[pl.ds(j * TOK, TOK), :]
             parts.append(dot(leavehot[j], rows).reshape(NDEV // 2, 8, HD))
         pair = jnp.stack([halves(parts[0], parts[1]), halves(parts[1], parts[0])], axis=1)
-        leaving[:, q] = pair.reshape(NDEV, 8, HD).astype(BF16)
+        leaving[pl.ds(0, NDEV), q] = pair.reshape(NDEV, 8, HD).astype(BF16)
 
     def send_back(q):
         for o in every:
@@ -402,12 +402,12 @@
             pltpu.VMEM((HEADS, TOK), I32),
             pltpu.VMEM((HEADS, TOK), I32),
             pltpu.VMEM((TOK, D), BF16),
-            pltpu.VMEM((HEADS, NSX, 4, 8, 2 * HD), BF16),
-            pltpu.VMEM((NDEV, 4, 8, 2 * HD), BF16),
-            pltpu.VMEM((NDEV, 4, 8, HD), BF16),
-            pltpu.VMEM((HEADS, NSX, 4, 8, HD), BF16),
-            pltpu.VMEM((HEADS, 1, TOK), I32),
-            pltpu.VMEM((NSY, 1, TOK), I32),
+            pltpu.VMEM((HEADS + 1, NSX, 4, 8, 2 * HD), BF16),
+            pltpu.VMEM((NDEV + 1, 4, 8, 2 * HD), BF16),
+            pltpu.VMEM((NDEV + 1, 4, 8, HD), BF16),
+            pltpu.VMEM((HEADS + 1, NSX, 4, 8, HD), BF16),
+            pltpu.VMEM((2 * HEADS, 1, TOK), I32),
+            pltpu.VMEM((2 * NSY, 1, TOK), I32),
             pltpu.VMEM((8, TOK), I32),
             pltpu.VMEM((8, TOK, 128), I32),
             pltpu.VMEM((8, TOK), I32),

time: 52.7 us -> 52.7 us (level)
  no operation moved by 1% of the time
where the time goes in v5:
time: 52.7 us; the launch traced here: 52.6 us
  Pallas kernels  50.3 us (95%)
  matrix products  2.23 us (4%)
    pallas_call x1, Pallas kernels, per_device(): pl.pallas_call(kernel, out_shape=jax.ShapeDtypeStruct((TOK, D), BF16), in...  50.3 us
    dot_general x1, matrix products, per_device(): return jnp.dot(merged, w_out, preferred_element_type=F32).astype(BF16)  2.23 us

profile of v5, /device:TPU:1, one launch (start us, length us, event | category | flops | bytes accessed | tf_op | source)
XLA Modules:
  0.0 52.6 jit_solution(5967006105346715074)
XLA Ops:
  0.0 0.0 copy-start
  0.0 50.3 %shard_map.73 = bf16[512,1024]{1,0:T(8,128)(2,1)S(1)} custom-call(bf16[512,1024]{1,0:T(8,128)(2,1)} %tokens_hbm.1, f32[1,1024]{1,0:T(1,128)} %bitcast.3, bf16[1024,1024]{1,0:T(8,128)(2,1)} %wqk_hbm.1, bf16[1024,1024]{1,0:T(8,128)(2,1)} %wv_hbm.1, s32[8,512]{1,0:T(8,128)} %send_hbm.1, s32[8,512]{1,0:T(8,128)} %place_hbm.1), custom_call_target="tpu_custom_call" | custom-call | tf_op jit(solution)/shard_map/pallas_call | solution.py:393
  50.3 0.0 copy-done
  50.4 2.2 %convolution_convert_fusion = bf16[512,1024]{1,0:T(8,128)(2,1)} fusion(bf16[512,1024]{1,0:T(8,128)(2,1)S(1)} %shard_map.73, bf16[1024,1024]{1,0:T(8,128)(2,1)S(1)} %copy-done), kind=kOutput, calls=%fused_computation | convolution fusion | flops 1074266112 | bytes 4194304 | tf_op jit(solution)/shard_map/dot_general | solution.py:435
Async XLA Ops:
  0.0 50.3 %copy-start = (bf16[1024,1024]{1,0:T(8,128)(2,1)S(1)}, bf16[1024,1024]{1,0:T(8,128)(2,1)}, u32[]{:S(2)}) copy-start(bf16[1024,1024]{1,0:T(8,128)(2,1)} %param.11) | copy-start | bytes 6291460
